TPU v7x, 32 devices: a whole 2x2x4 slice. The times are simulated.
32 devices in a mesh: lat: 16 (over z, x, core), lev: 2 (over y).
Axes of the slice: x: 2, y: 2, z: 4, core: 2. Of those that a mesh axis runs over, the one named last changes fastest.
Arguments:
- anomalies: bfloat16 [4, 2, 80, 32, 1536], P(None, 'lev', None, 'lat'), may hold values from -6 to 6
- error_now: float32 [4, 2, 32, 1536], P(None, 'lev', 'lat'), may hold values from -6 to 6
- error_prior: float32 [4, 2, 32, 1536], P(None, 'lev', 'lat'), may hold values from -4.2 to 4.2
- energy_coef: float32 [4, 2], P(None, 'lev'), may hold values from 0.3 to 3
- obs_anomalies: bfloat16 [2048, 80, 256], P('lat', 'lev'), may hold values from -6 to 6
- innovations: float32 [2048, 256], P('lat'), may hold values from -6 to 6
- valid_counts: int32 [2048], P('lat'), may hold values from 0 to 256, as said below
- type_ids: int32 [2048], P('lat'), may hold values from 0 to 7
- error_inverse: float32 [8], replicated, may hold values from 0.25 to 4
Outputs:
- impact: float32 [2048, 16, 256], P('lat', 'lev')
- type_totals: float32 [16, 8], P('lev')
Inputs may be any that keep to these rules, and one draw needn't show every extreme that they name: `valid_counts`: among the 128 slots of each index of lat, the blocks with a positive count come first and the first is always positive; in every draw some index of lat has all 128 slots positive and some block holds 256 rows. Rows below a block's count are observations, the rest padding.
All inputs are finite; a program needn't handle non-finite values.
Results may differ from a plain program's by a relative error of at most 0.0042.
Values may be sent and summed in bfloat16 or wider, within the bound.
No kernel may reach another device: no remote copies, remote signals or barrier semaphores. Data moves between devices by JAX's collectives and lax.ppermute only.
A program may use at most 64 MiB of HBM per device.

v0:
```python
import math

import jax
import jax.numpy as jnp
from jax import lax
from jax.sharding import PartitionSpec as P

NLAT_GRID = 768
LAT0 = 256
REGIONS = 4
NTYPES = 8


def local(
    anomalies,
    error_now,
    error_prior,
    energy_coef,
    obs_anomalies,
    innovations,
    valid_counts,
    type_ids,
    error_inverse,
):
    lat_rows = error_now.shape[2]
    lat_total = lat_rows * lax.axis_size("lat")
    lev_total = error_now.shape[1] * lax.axis_size("lev")
    lon_count = error_now.shape[3]
    lat_index = lax.axis_index("lat") * lat_rows + jnp.arange(lat_rows, dtype=jnp.int32)
    cosine = jnp.cos(
        -0.5 * math.pi + ((lat_index + LAT0).astype(jnp.float32) + 0.5) * math.pi / NLAT_GRID
    )
    gradient = (
        energy_coef[:, :, None, None] * cosine[None, None, :, None] * (error_now + error_prior)
    ).astype(jnp.bfloat16)
    folded = jnp.einsum("vlkji,vlji->vkj", anomalies, gradient, preferred_element_type=jnp.float32)
    region = lat_index * REGIONS // lat_total
    onehot = (region[None, :] == jnp.arange(REGIONS, dtype=jnp.int32)[:, None]).astype(jnp.float32)
    partial_value = jnp.einsum("vkj,rj->vkr", folded, onehot, precision=lax.Precision.HIGHEST)
    summed = lax.psum(partial_value, ("lat", "lev"))
    members = anomalies.shape[2]
    norm_scale = math.sqrt(lev_total * lat_total * lon_count / REGIONS)
    weights = (jnp.transpose(summed, (1, 0, 2)).reshape(members, -1) / norm_scale).astype(
        jnp.bfloat16
    )
    slot_count, local_members, block_rows = obs_anomalies.shape
    lev_groups = lax.axis_size("lev")
    grouped = obs_anomalies.reshape(lev_groups, slot_count // lev_groups, local_members, block_rows)
    answered = jnp.einsum(
        "gbks,kt->gbts",
        lax.all_to_all(grouped, "lev", split_axis=0, concat_axis=2, tiled=True),
        weights,
        preferred_element_type=jnp.float32,
    )
    response = lax.all_to_all(answered[0], "lev", split_axis=1, concat_axis=0, tiled=True)
    type_table = type_ids[:, None] == jnp.arange(NTYPES, dtype=jnp.int32)[None, :]
    inverse_var = jnp.sum(
        jnp.where(type_table, error_inverse[None, :], jnp.zeros((), jnp.float32)), axis=1
    )
    positions = jnp.arange(block_rows, dtype=jnp.int32)
    row_mask = (positions[None, :] < valid_counts[:, None]).astype(jnp.float32)
    scaling = innovations * inverse_var[:, None] * row_mask / math.sqrt(members - 1)
    impact = response * scaling[:, None, :]
    per_block = jnp.sum(impact, axis=2)
    local_totals = jnp.dot(
        per_block.T, type_table.astype(jnp.float32), precision=lax.Precision.HIGHEST
    )
    block_total = slot_count * lax.axis_size("lat")
    type_totals = lax.psum(local_totals, "lat") / math.sqrt(block_total * block_rows / NTYPES)
    return (impact, type_totals)


def solution(mesh):
    in_specs = (
        P(None, "lev", None, "lat", None),
        P(None, "lev", "lat", None),
        P(None, "lev", "lat", None),
        P(None, "lev"),
        P("lat", "lev", None),
        P("lat", None),
        P("lat"),
        P("lat"),
        P(),
    )
    out_specs = (P("lat", "lev", None), P("lev", None))
    return jax.shard_map(local, mesh=mesh, in_specs=in_specs, out_specs=out_specs, check_vma=False)
```

profile of v0, /device:TPU:0, one launch (start us, length us, event | category | flops | bytes accessed | tf_op | source)
XLA Modules:
  0.0 126.0 jit_solution(2320645867197905039)
XLA Ops:
  0.6 0.0 copy-start
  0.7 5.2 %all-to-all-start = ((bf16[2,64,40,256]{3,2,1,0:T(8,128)(2,1)}), bf16[2,64,40,256]{3,2,1,0:T(8,128)(2,1)}, u32[]{:S(2)}, u32[]{:S(2)}) async-start(bf16[2,64,40,256]{3,2,1,0:T(8,128)(2,1)} %bitcast.48), calls=%async_computation | async-start | bytes 5242880 | tf_op jit(solution)/shard_map/all_to_all | solution.py:51
  5.9 0.1 broadcast_multiply_fusion.1
  6.0 0.1 fusion.4
  6.1 0.6 fusion
  6.7 0.3 fusion.7
  7.0 65.6 %psum.14 = f32[4,80,4]{1,2,0:T(4,128)S(1)} all-reduce(f32[4,80,4]{1,2,0:T(4,128)S(1)} %fusion.7), channel_id=1, replica_groups=mesh['lat'=16,'lev'=2] {'lat','lev'}, use_global_device_ids=true, to_apply=%region_0.1 | all-reduce | flops 1280 | bytes 10240 | tf_op jit(solution)/shard_map/psum | solution.py:40
  72.5 1.9 %copy.25 = bf16[1,64,2,40,256]{4,3,2,1,0:T(8,128)(2,1)S(1)} copy(bf16[1,64,2,40,256]{4,3,1,2,0:T(8,128)(2,1)} %bitcast.13) | data formatting | bytes 5242880 | tf_op jit(solution)/shard_map/all_to_all | solution.py:51
  74.5 0.5 convolution_bitcast_fusion
  74.9 0.0 copy-start.1
  75.0 1.6 %copy.26 = f32[64,16,256]{2,0,1:T(8,128)} copy(f32[64,16,256]{2,1,0:T(8,128)S(1)} %convolution_bitcast_fusion) | data formatting | bytes 2097152 | tf_op jit(solution)/shard_map/squeeze | solution.py:55
  76.6 3.6 %all-to-all-start.1 = ((f32[64,16,256]{2,0,1:T(8,128)}), f32[64,16,256]{2,0,1:T(8,128)S(1)}, u32[]{:S(2)}, u32[]{:S(2)}) async-start(f32[64,16,256]{2,0,1:T(8,128)} %copy.26), calls=%async_computation.1 | async-start | bytes 2097152 | tf_op jit(solution)/shard_map/all_to_all | solution.py:55
  80.2 0.1 select_reduce_fusion
  80.3 0.1 select_multiply_fusion
  80.4 0.1 copy.29
  80.5 12.7 %all-to-all-done.1 = f32[64,16,256]{2,0,1:T(8,128)S(1)} async-done(((f32[64,16,256]{2,0,1:T(8,128)}), f32[64,16,256]{2,0,1:T(8,128)S(1)}, u32[]{:S(2)}, u32[]{:S(2)}) %all-to-all-start.1) | async-done | bytes 1048608 | tf_op jit(solution)/shard_map/all_to_all | solution.py:55
  93.2 0.7 fusion.2
  93.9 0.1 copy.30
  94.0 0.1 reduce_sum.22
  94.1 0.1 fusion.5
  94.2 29.5 %psum.15 = f32[8,8]{1,0:T(8,128)S(1)} all-reduce(f32[8,8]{1,0:T(8,128)S(1)} %fusion.5), channel_id=1, replica_groups=mesh['lat'=16,'lev'=2] {'lat'}, use_global_device_ids=true, to_apply=%region_3.4 | all-reduce | flops 64 | bytes 512 | tf_op jit(solution)/shard_map/psum | solution.py:69
  123.7 0.6 broadcast_multiply_fusion
  124.3 0.6 copy.28
  124.9 1.1 bitcast_multiply_fusion
  (18 shorter events, 0.1 us)
Async XLA Ops:
  0.6 5.5 %copy-start = (bf16[4,1,80,2,1536]{4,3,2,1,0:T(2,128)(2,1)S(1)}, bf16[4,1,80,2,1536]{4,3,2,1,0:T(2,128)(2,1)}, u32[]{:S(2)}) copy-start(bf16[4,1,80,2,1536]{4,3,2,1,0:T(2,128)(2,1)} %param.9) | copy-start | bytes 5898244
  0.6 5.3 %copy-start.6 = (f32[4,1]{0,1:T(1,128)S(1)}, f32[4,1]{0,1:T(1,128)}, u32[]{:S(2)}) copy-start(f32[4,1]{0,1:T(1,128)} %param.12) | copy-start | bytes 52
  0.7 5.3 %copy-start.2 = (f32[4,1,2,1536]{3,2,1,0:T(2,128)S(1)}, f32[4,1,2,1536]{3,2,1,0:T(2,128)}, u32[]{:S(2)}) copy-start(f32[4,1,2,1536]{3,2,1,0:T(2,128)} %param.10) | copy-start | bytes 147460
  0.7 5.3 %copy-start.3 = (f32[4,1,2,1536]{3,2,1,0:T(2,128)S(1)}, f32[4,1,2,1536]{3,2,1,0:T(2,128)}, u32[]{:S(2)}) copy-start(f32[4,1,2,1536]{3,2,1,0:T(2,128)} %param.11) | copy-start | bytes 147460
  0.7 71.9 %all-to-all-start = ((bf16[2,64,40,256]{3,2,1,0:T(8,128)(2,1)}), bf16[2,64,40,256]{3,2,1,0:T(8,128)(2,1)}, u32[]{:S(2)}, u32[]{:S(2)}) async-start(bf16[2,64,40,256]{3,2,1,0:T(8,128)(2,1)} %bitcast.48), calls=%async_computation | async-start | bytes 5242880 | tf_op jit(solution)/shard_map/all_to_all | solution.py:51
  74.9 5.2 %copy-start.5 = (s32[128]{0:T(128)S(1)}, s32[128]{0:T(128)}, u32[]{:S(2)}) copy-start(s32[128]{0:T(128)} %param.16) | copy-start | bytes 1540
  74.9 5.2 %copy-start.7 = (f32[8]{0:T(128)S(1)}, f32[8]{0:T(128)}, u32[]{:S(2)}) copy-start(f32[8]{0:T(128)} %param.17) | copy-start | bytes 100
  74.9 5.3 %copy-start.1 = (f32[128,256]{1,0:T(8,128)S(1)}, f32[128,256]{1,0:T(8,128)}, u32[]{:S(2)}) copy-start(f32[128,256]{1,0:T(8,128)} %param.14) | copy-start | bytes 393220
  75.0 5.3 %copy-start.4 = (s32[128]{0:T(128)S(1)}, s32[128]{0:T(128)}, u32[]{:S(2)}) copy-start(s32[128]{0:T(128)} %param.15) | copy-start | bytes 1540
  76.6 16.6 %all-to-all-start.1 = ((f32[64,16,256]{2,0,1:T(8,128)}), f32[64,16,256]{2,0,1:T(8,128)S(1)}, u32[]{:S(2)}, u32[]{:S(2)}) async-start(f32[64,16,256]{2,0,1:T(8,128)} %copy.26), calls=%async_computation.1 | async-start | bytes 2097152 | tf_op jit(solution)/shard_map/all_to_all | solution.py:55
where the time goes:
time: 126 us
  blocking collectives  95 us (75%)
  waiting for transfers between devices  12.7 us (10%)
  starting transfers between devices  8.74 us (7%)
  local copies, waits for them, and re-layouts  4.43 us (4%)
  other arithmetic  2.83 us (2%)
  matrix products  1.44 us (1%)
    psum x1, blocking collectives, local(): summed = lax.psum(partial_value, ('lat', 'lev'))  65.6 us
    psum x1, blocking collectives, local(): lax.psum(local_totals, 'lat') / math.sqrt(block_total * block_rows / NTYPES)  29.5 us
    all_to_all x1, waiting for transfers between devices, local(): lax.all_to_all(answered[0], 'lev', split_axis=1, concat_axis=0, tiled=True)  12.7 us
    all_to_all x1, starting transfers between devices, local(): lax.all_to_all(grouped, 'lev', split_axis=0, concat_axis=2, tiled=True)  5.16 us
    all_to_all x1, starting transfers between devices, local(): lax.all_to_all(answered[0], 'lev', split_axis=1, concat_axis=0, tiled=True)  3.58 us
  transfers between devices with their start and end apart: 2, of which 1 were waited for; matrix products, arithmetic and copies ran while one was open for 1% of the time, Pallas kernels for 0%

commit v1 on v0

v1 whole, which is shorter than its diff:
```python
import math

import jax
import jax.numpy as jnp
from jax import lax
from jax.sharding import PartitionSpec as P

NLAT_GRID = 768
LAT0 = 256
REGIONS = 4
NTYPES = 8


def exchange(value, axis, bit):
    size = lax.axis_size(axis)
    return lax.ppermute(value, axis, [(i, i ^ bit) for i in range(size)])


def butterfly(value, axis):
    bit = 1
    while bit < lax.axis_size(axis):
        value = value + exchange(value, axis, bit)
        bit *= 2
    return value


def local(
    anomalies,
    error_now,
    error_prior,
    energy_coef,
    obs_anomalies,
    innovations,
    valid_counts,
    type_ids,
    error_inverse,
):
    lat_rows = error_now.shape[2]
    lat_total = lat_rows * lax.axis_size("lat")
    lev_total = error_now.shape[1] * lax.axis_size("lev")
    lon_count = error_now.shape[3]
    variables = anomalies.shape[0]
    members = anomalies.shape[2]
    slot_count, local_members, block_rows = obs_anomalies.shape
    levs = lax.axis_size("lev")
    lev_index = lax.axis_index("lev")
    targets = variables * REGIONS
    own_targets = targets // levs

    lat_index = lax.axis_index("lat") * lat_rows + jnp.arange(lat_rows, dtype=jnp.int32)
    cosine = jnp.cos(
        -0.5 * math.pi + ((lat_index + LAT0).astype(jnp.float32) + 0.5) * math.pi / NLAT_GRID
    )
    gradient = (
        energy_coef[:, :, None, None] * cosine[None, None, :, None] * (error_now + error_prior)
    ).astype(jnp.bfloat16)
    folded = jnp.einsum("vlkji,vlji->vkj", anomalies, gradient, preferred_element_type=jnp.float32)
    region = lat_index * REGIONS // lat_total
    onehot = (region[None, :] == jnp.arange(REGIONS, dtype=jnp.int32)[:, None]).astype(jnp.float32)
    partial = jnp.einsum("vkj,rj->vrk", folded, onehot, precision=lax.Precision.HIGHEST)
    partial = butterfly(partial.reshape(targets, members), "lev")
    own = lax.dynamic_slice_in_dim(partial, lev_index * local_members, local_members, axis=1)

    type_table = type_ids[:, None] == jnp.arange(NTYPES, dtype=jnp.int32)[None, :]
    inverse_var = jnp.sum(
        jnp.where(type_table, error_inverse[None, :], jnp.zeros((), jnp.float32)), axis=1
    )
    positions = jnp.arange(block_rows, dtype=jnp.int32)
    row_mask = (positions[None, :] < valid_counts[:, None]).astype(jnp.float32)
    scaling = innovations * inverse_var[:, None] * row_mask / math.sqrt(members - 1)
    per_block = jnp.sum(obs_anomalies.astype(jnp.float32) * scaling[:, None, :], axis=2)
    per_type = jnp.einsum(
        "bc,bk->ck", type_table.astype(jnp.float32), per_block, precision=lax.Precision.HIGHEST
    )

    summed = butterfly(jnp.concatenate([own, per_type], axis=0), "lat")
    norm_scale = math.sqrt(lev_total * lat_total * lon_count / REGIONS)
    weights = (summed[:targets] / norm_scale).astype(jnp.bfloat16)
    per_type = summed[targets:]

    weight_parts = weights.reshape(levs, own_targets, local_members)
    total_parts = jnp.einsum(
        "tk,ck->tc", weights.astype(jnp.float32), per_type, precision=lax.Precision.HIGHEST
    ).reshape(levs, own_targets, NTYPES)

    def respond(part):
        return jnp.einsum(
            "bks,tk->bts", obs_anomalies, part, preferred_element_type=jnp.float32
        )

    def pick(parts, index):
        return lax.dynamic_index_in_dim(parts, index, 0, keepdims=False)

    received = []
    total_received = []
    for step in range(1, levs):
        perm = [(i, (i + step) % levs) for i in range(levs)]
        peer = (lev_index + step) % levs
        sent = respond(pick(weight_parts, peer)).astype(jnp.bfloat16)
        received.append(lax.ppermute(sent, "lev", perm))
        total_received.append(lax.ppermute(pick(total_parts, peer), "lev", perm))
    response = respond(pick(weight_parts, lev_index))
    for part in received:
        response = response + part.astype(jnp.float32)
    impact = response * scaling[:, None, :]
    totals = pick(total_parts, lev_index)
    for part in total_received:
        totals = totals + part
    block_total = slot_count * lax.axis_size("lat")
    type_totals = totals / math.sqrt(block_total * block_rows / NTYPES)
    return (impact, type_totals)


def solution(mesh):
    in_specs = (
        P(None, "lev", None, "lat", None),
        P(None, "lev", "lat", None),
        P(None, "lev", "lat", None),
        P(None, "lev"),
        P("lat", "lev", None),
        P("lat", None),
        P("lat"),
        P("lat"),
        P(),
    )
    out_specs = (P("lat", "lev", None), P("lev", None))
    return jax.shard_map(local, mesh=mesh, in_specs=in_specs, out_specs=out_specs, check_vma=False)
```

time: 126 us -> 40 us (0.32)
  blocking collectives: 95 us -> 0 us
  matrix products: 1.44 us -> 6.75 us
  local copies, waits for them, and re-layouts: 4.43 us -> 0.26 us
  waiting for transfers between devices: 12.7 us -> 15.7 us
  other arithmetic: 2.83 us -> 5.51 us
  starting transfers between devices: 8.74 us -> 10.8 us
    psum x2 -> x0, blocking collectives: 95 us -> none  [the longest x1 65.6 us: local(): summed = lax.psum(partial_value, ('lat', 'lev'))]
    ppermute x0 -> x7, waiting for transfers between devices: none -> 15.7 us  [the longest x1 8.24 us: local(): total_received.append(lax.ppermute(pick(total_parts, peer), 'lev', perm))]
    all_to_all x2 -> x0, waiting for transfers between devices: 12.7 us -> none  [the longest x1 12.7 us: local(): lax.all_to_all(answered[0], 'lev', split_axis=1, concat_axis=0, tiled=True)]
    ppermute x0 -> x7, starting transfers between devices: none -> 10.8 us  [the longest x5 8.68 us: exchange(): return lax.ppermute(value, axis, [(i, i ^ bit) for i in range(size)])]
    all_to_all x2 -> x0, starting transfers between devices: 8.74 us -> none  [the longest x1 5.16 us: local(): lax.all_to_all(grouped, 'lev', split_axis=0, concat_axis=2, tiled=True)]
    dot_general x3 -> x5, matrix products: 0.83 us -> 6.14 us  [the longest x2 5.61 us: respond(): jnp.einsum('bks,tk->bts', obs_anomalies, part, preferred_element_type=jnp...]
    all_to_all x2 -> x0, local copies, waits for them, and re-layouts: 2.55 us -> none  [the longest x1 1.94 us: local(): lax.all_to_all(grouped, 'lev', split_axis=0, concat_axis=2, tiled=True)]
    squeeze x1 -> x0, local copies, waits for them, and re-layouts: 1.58 us -> none  [local(): answered[0]]
  transfers between devices with their start and end apart: 2 -> 7, of which waited for: 1 -> 5; matrix products, arithmetic and copies ran while one was open for 1% -> 9% of each run, Pallas kernels for 0% -> 0%
where the time goes in v1:
time: 40 us; the launch traced here: 39.8 us
  waiting for transfers between devices  15.7 us (39%)
  starting transfers between devices  10.8 us (27%)
  matrix products  6.75 us (17%)
  other arithmetic  5.51 us (14%)
  between operations  0.74 us (2%)
    ppermute x5, starting transfers between devices, exchange(): return lax.ppermute(value, axis, [(i, i ^ bit) for i in range(size)])  8.68 us
    ppermute x1, waiting for transfers between devices, local(): total_received.append(lax.ppermute(pick(total_parts, peer), 'lev', perm))  8.24 us
    ppermute x5, waiting for transfers between devices, exchange(): return lax.ppermute(value, axis, [(i, i ^ bit) for i in range(size)])  7.49 us
    dot_general x2, matrix products, respond(): jnp.einsum('bks,tk->bts', obs_anomalies, part, preferred_element_type=jnp...  5.61 us
    another operation x1, other arithmetic  1.33 us
    ppermute x1, starting transfers between devices, local(): total_received.append(lax.ppermute(pick(total_parts, peer), 'lev', perm))  1.11 us
    div x1, other arithmetic, local(): innovations * inverse_var[:, None] * row_mask / math.sqrt(members - 1)  1 us
    ppermute x1, starting transfers between devices, local(): received.append(lax.ppermute(sent, 'lev', perm))  0.99 us
  transfers between devices with their start and end apart: 7, of which 5 were waited for; matrix products, arithmetic and copies ran while one was open for 9% of the time, Pallas kernels for 0%

profile of v1, /device:TPU:0, one launch (start us, length us, event | category | flops | bytes accessed | tf_op | source)
XLA Modules:
  0.0 39.8 jit_solution(3555212215820313965)
XLA Ops:
  0.7 0.9 %broadcast_multiply_fusion = f32[4,2]{1,0:T(4,128)S(1)} fusion(f32[2]{0:T(128)S(1)} %add_cosine_fusion, f32[4]{0:T(128)} %bitcast.48), kind=kLoop, calls=%fused_computation.40 | loop fusion | flops 8 | bytes 56 | tf_op jit(solution)/shard_map/mul | solution.py:55
  1.6 1.3 %fusion.4 = bf16[4,2,1536,1]{2,1,0,3:T(2,128)(2,1)S(1)} fusion(f32[4,1,2,1536]{3,2,1,0:T(2,128)} %param.10, f32[4,1,2,1536]{3,2,1,0:T(2,128)} %param.11, f32[4,2]{1,0:T(4,128)S(1)} %broadcast_multiply_fusion), kind=kLoop, calls=%fused_computation.11 | loop fusion | flops 36864 | bytes 122912 | tf_op jit(solution)/shard_map/reshape.6
  3.0 0.6 %fusion = f32[4,2,1,80]{3,2,1,0:T(1,128)S(1)} fusion(bf16[4,80,2,1536]{3,2,1,0:T(2,128)(2,1)S(1)} %bitcast.44, bf16[4,2,1536,1]{2,1,0,3:T(2,128)(2,1)S(1)} %fusion.4), kind=kOutput, calls=%fused_computation.1 | convolution fusion | flops 1966080 | bytes 1993216 | tf_op jit(solution)/shard_map/vlkji,vlji->vkj/dot_general | solution.py:57
  3.6 0.3 fusion.17
  3.8 3.0 %collective-permute-start = (f32[16,80]{1,0:T(8,128)S(1)}, f32[16,80]{1,0:T(8,128)S(1)}, u32[]{:S(2)}, u32[]{:S(2)}) collective-permute-start(f32[16,80]{1,0:T(8,128)S(1)} %bitcast.45), channel_id=1, source_target_pairs={{0,1},{1,0},{2,3},{3,2},{4,5},{5,4},{6,7},{7,6},{8,9},{9,8},{10,11... | collective-permute-start | bytes 15368 | tf_op jit(solution)/shard_map/ppermute | solution.py:16
  6.8 0.8 %select_reduce_fusion = f32[128]{0:T(128)S(1)} fusion(f32[8]{0:T(128)} %param.17, s32[128]{0:T(128)} %param.16), kind=kLoop, calls=%fused_computation.20 | loop fusion | flops 2944 | bytes 1056 | tf_op jit(solution)/shard_map/reduce_sum | solution.py:65
  7.6 1.0 %select_multiply_fusion = f32[128,256]{1,0:T(8,128)S(1)} fusion(f32[128,256]{1,0:T(8,128)} %param.14, f32[128]{0:T(128)S(1)} %select_reduce_fusion, s32[128]{0:T(128)} %param.15), kind=kLoop, calls=%fused_computation.7 | loop fusion | flops 131072 | bytes 263168 | tf_op jit(solution)/shard_map/div | solution.py:70
  8.6 0.8 %multiply_reduce_fusion = f32[128,40]{1,0:T(8,128)S(1)} fusion(bf16[128,40,256]{2,1,0:T(8,128)(2,1)S(1)} %copy-done.1, f32[128,256]{1,0:T(8,128)S(1)} %select_multiply_fusion), kind=kLoop, calls=%fused_computation | loop fusion | flops 3927040 | bytes 2772992 | tf_op jit(solution)/shard_map/reduce_sum | solution.py:71
  9.4 0.1 fusion.9
  9.5 0.1 dynamic-slice_add_fusion
  9.7 1.2 %collective-permute-done.1 = f32[24,40]{1,0:T(8,128)S(1)} collective-permute-done((f32[24,40]{1,0:T(8,128)S(1)}, f32[24,40]{1,0:T(8,128)S(1)}, u32[]{:S(2)}, u32[]{:S(2)}) %collective-permute-start.1) | collective-permute-done | bytes 3872 | tf_op jit(solution)/shard_map/ppermute | solution.py:16
  10.8 1.5 %collective-permute-start.2 = (f32[24,40]{1,0:T(8,128)S(1)}, f32[24,40]{1,0:T(8,128)S(1)}, u32[]{:S(2)}, u32[]{:S(2)}) collective-permute-start(f32[24,40]{1,0:T(8,128)S(1)} %fusion.27), channel_id=1, source_target_pairs={{0,4},{2,6},{4,0},{6,2},{8,12},{10,14},{12,8},{14,10},{16,20},{18,... | collective-permute-start | bytes 11528 | tf_op jit(solution)/shard_map/ppermute | solution.py:16
  12.3 2.2 %collective-permute-done.2 = f32[24,40]{1,0:T(8,128)S(1)} collective-permute-done((f32[24,40]{1,0:T(8,128)S(1)}, f32[24,40]{1,0:T(8,128)S(1)}, u32[]{:S(2)}, u32[]{:S(2)}) %collective-permute-start.2) | collective-permute-done | bytes 3872 | tf_op jit(solution)/shard_map/ppermute | solution.py:16
  14.5 1.6 %collective-permute-start.3 = (f32[24,40]{1,0:T(8,128)S(1)}, f32[24,40]{1,0:T(8,128)S(1)}, u32[]{:S(2)}, u32[]{:S(2)}) collective-permute-start(f32[24,40]{1,0:T(8,128)S(1)} %add.93), channel_id=1, source_target_pairs={{0,8},{2,10},{4,12},{6,14},{8,0},{10,2},{12,4},{14,6},{16,24},{18,... | collective-permute-start | bytes 11528 | tf_op jit(solution)/shard_map/ppermute | solution.py:16
  16.1 2.1 %collective-permute-done.3 = f32[24,40]{1,0:T(8,128)S(1)} collective-permute-done((f32[24,40]{1,0:T(8,128)S(1)}, f32[24,40]{1,0:T(8,128)S(1)}, u32[]{:S(2)}, u32[]{:S(2)}) %collective-permute-start.3) | collective-permute-done | bytes 3872 | tf_op jit(solution)/shard_map/ppermute | solution.py:16
  18.2 2.6 %collective-permute-start.4 = (f32[24,40]{1,0:T(8,128)S(1)}, f32[24,40]{1,0:T(8,128)S(1)}, u32[]{:S(2)}, u32[]{:S(2)}) collective-permute-start(f32[24,40]{1,0:T(8,128)S(1)} %add.94), channel_id=1, source_target_pairs={{0,16},{2,18},{4,20},{6,22},{8,24},{10,26},{12,28},{14,30},{16,0},... | collective-permute-start | bytes 11528 | tf_op jit(solution)/shard_map/ppermute | solution.py:16
  20.8 2.0 %collective-permute-done.4 = f32[24,40]{1,0:T(8,128)S(1)} collective-permute-done((f32[24,40]{1,0:T(8,128)S(1)}, f32[24,40]{1,0:T(8,128)S(1)}, u32[]{:S(2)}, u32[]{:S(2)}) %collective-permute-start.4) | collective-permute-done | bytes 3872 | tf_op jit(solution)/shard_map/ppermute | solution.py:16
  22.8 2.3 %fusion.2 = bf16[128,8,256]{2,1,0:T(8,128)(2,1)S(1)} fusion(bf16[128,40,256]{2,1,0:T(8,128)(2,1)} %param.13, bf16[2,8,40]{2,1,0:T(8,128)(2,1)S(1)} %fusion.23, s32[]{:T(128)S(6)} %select_n.38), kind=kOutput, calls=%fused_computation.5 | convolution fusion | flops 21233664 | bytes 3147780 | tf_op jit(solution)/shard_map/bks,tk->bts/dot_general | solution.py:87
  25.2 1.0 %collective-permute-start.5 = (bf16[128,8,256]{2,1,0:T(8,128)(2,1)S(1)}, bf16[128,8,256]{2,1,0:T(8,128)(2,1)S(1)}, u32[]{:S(2)}, u32[]{:S(2)}) collective-permute-start(bf16[128,8,256]{2,1,0:T(8,128)(2,1)S(1)} %fusion.2), channel_id=1, source_target_pairs={{0,1},{1,0},{2,3},{3,2},{4,5},{5,4},{6,7},{7,6},{8,9},{9,8},{10,11... | collective-permute-start | bytes 1572872 | tf_op jit(solution)/shard_map/ppermute | solution.py:100
  26.2 0.1 fusion.6
  26.4 1.1 %collective-permute-start.6 = (f32[8,8]{1,0:T(8,128)S(1)}, f32[8,8]{1,0:T(8,128)S(1)}, u32[]{:S(2)}, u32[]{:S(2)}) collective-permute-start(f32[8,8]{1,0:T(8,128)S(1)} %bitcast.47), channel_id=1, source_target_pairs={{0,1},{1,0},{2,3},{3,2},{4,5},{5,4},{6,7},{7,6},{8,9},{9,8},{10,11... | collective-permute-start | bytes 776 | tf_op jit(solution)/shard_map/ppermute | solution.py:101
  27.6 8.2 %collective-permute-done.6 = f32[8,8]{1,0:T(8,128)S(1)} collective-permute-done((f32[8,8]{1,0:T(8,128)S(1)}, f32[8,8]{1,0:T(8,128)S(1)}, u32[]{:S(2)}, u32[]{:S(2)}) %collective-permute-start.6) | collective-permute-done | bytes 288 | tf_op jit(solution)/shard_map/ppermute | solution.py:101
  35.9 0.6 %fusion.8 = f32[8,8]{1,0:T(8,128)} fusion(f32[8,8]{1,0:T(8,128)S(1)} %collective-permute-done.6, f32[1,8,8]{2,1,0:T(8,128)S(1)} %copy.13), kind=kLoop, calls=%fused_computation.19 | loop fusion | flops 128 | bytes 768 | tf_op jit(solution)/shard_map/div | solution.py:110
  36.5 3.3 %add_multiply_fusion = f32[128,8,256]{2,1,0:T(8,128)} fusion(bf16[128,8,256]{2,1,0:T(8,128)(2,1)S(1)} %collective-permute-done.5, f32[128,256]{1,0:T(8,128)S(1)} %select_multiply_fusion, bf16[128,40,256]{2,1,0:T(8,128)(2,1)} %param.13, bf16[2,8,40]{2,1,0:T(8,128)(2,1)S(1)} %fusion.23, s32[]{:T(128)S(6)} %select_n.36), kind=kOutput, calls=%fused_computation.6 | convolution fusion | flops 21757952 | bytes 4327428 | tf_op jit(solution)/shard_map/bks,tk->bts/dot_general | solution.py:87
  (21 shorter events, 0.4 us)
Async XLA Ops:
  0.6 2.3 %copy-start = (bf16[4,1,80,2,1536]{4,3,2,1,0:T(2,128)(2,1)S(1)}, bf16[4,1,80,2,1536]{4,3,2,1,0:T(2,128)(2,1)}, u32[]{:S(2)}) copy-start(bf16[4,1,80,2,1536]{4,3,2,1,0:T(2,128)(2,1)} %param.9) | copy-start | bytes 5898244
  0.6 8.0 %copy-start.1 = (bf16[128,40,256]{2,1,0:T(8,128)(2,1)S(1)}, bf16[128,40,256]{2,1,0:T(8,128)(2,1)}, u32[]{:S(2)}) copy-start(bf16[128,40,256]{2,1,0:T(8,128)(2,1)} %param.13) | copy-start | bytes 7864324
  2.9 6.5 %copy-start.2 = (s32[128]{0:T(128)S(1)}, s32[128]{0:T(128)}, u32[]{:S(2)}) copy-start(s32[128]{0:T(128)} %param.16) | copy-start | bytes 1540
  3.8 5.7 %collective-permute-start = (f32[16,80]{1,0:T(8,128)S(1)}, f32[16,80]{1,0:T(8,128)S(1)}, u32[]{:S(2)}, u32[]{:S(2)}) collective-permute-start(f32[16,80]{1,0:T(8,128)S(1)} %bitcast.45), channel_id=1, source_target_pairs={{0,1},{1,0},{2,3},{3,2},{4,5},{5,4},{6,7},{7,6},{8,9},{9,8},{10,11... | collective-permute-start | bytes 15368 | tf_op jit(solution)/shard_map/ppermute | solution.py:16
  9.6 1.2 %collective-permute-start.1 = (f32[24,40]{1,0:T(8,128)S(1)}, f32[24,40]{1,0:T(8,128)S(1)}, u32[]{:S(2)}, u32[]{:S(2)}) collective-permute-start(f32[24,40]{1,0:T(8,128)S(1)} %pad_maximum_fusion), channel_id=1, source_target_pairs={{0,2},{2,0},{4,6},{6,4},{8,10},{10,8},{12,14},{14,12},{16,18},{18,... | collective-permute-start | bytes 11528 | tf_op jit(solution)/shard_map/ppermute | solution.py:16
  10.8 3.7 %collective-permute-start.2 = (f32[24,40]{1,0:T(8,128)S(1)}, f32[24,40]{1,0:T(8,128)S(1)}, u32[]{:S(2)}, u32[]{:S(2)}) collective-permute-start(f32[24,40]{1,0:T(8,128)S(1)} %fusion.27), channel_id=1, source_target_pairs={{0,4},{2,6},{4,0},{6,2},{8,12},{10,14},{12,8},{14,10},{16,20},{18,... | collective-permute-start | bytes 11528 | tf_op jit(solution)/shard_map/ppermute | solution.py:16
  14.5 3.7 %collective-permute-start.3 = (f32[24,40]{1,0:T(8,128)S(1)}, f32[24,40]{1,0:T(8,128)S(1)}, u32[]{:S(2)}, u32[]{:S(2)}) collective-permute-start(f32[24,40]{1,0:T(8,128)S(1)} %add.93), channel_id=1, source_target_pairs={{0,8},{2,10},{4,12},{6,14},{8,0},{10,2},{12,4},{14,6},{16,24},{18,... | collective-permute-start | bytes 11528 | tf_op jit(solution)/shard_map/ppermute | solution.py:16
  18.2 4.6 %collective-permute-start.4 = (f32[24,40]{1,0:T(8,128)S(1)}, f32[24,40]{1,0:T(8,128)S(1)}, u32[]{:S(2)}, u32[]{:S(2)}) collective-permute-start(f32[24,40]{1,0:T(8,128)S(1)} %add.94), channel_id=1, source_target_pairs={{0,16},{2,18},{4,20},{6,22},{8,24},{10,26},{12,28},{14,30},{16,0},... | collective-permute-start | bytes 11528 | tf_op jit(solution)/shard_map/ppermute | solution.py:16
  25.2 11.3 %collective-permute-start.5 = (bf16[128,8,256]{2,1,0:T(8,128)(2,1)S(1)}, bf16[128,8,256]{2,1,0:T(8,128)(2,1)S(1)}, u32[]{:S(2)}, u32[]{:S(2)}) collective-permute-start(bf16[128,8,256]{2,1,0:T(8,128)(2,1)S(1)} %fusion.2), channel_id=1, source_target_pairs={{0,1},{1,0},{2,3},{3,2},{4,5},{5,4},{6,7},{7,6},{8,9},{9,8},{10,11... | collective-permute-start | bytes 1572872 | tf_op jit(solution)/shard_map/ppermute | solution.py:100
  26.4 9.4 %collective-permute-start.6 = (f32[8,8]{1,0:T(8,128)S(1)}, f32[8,8]{1,0:T(8,128)S(1)}, u32[]{:S(2)}, u32[]{:S(2)}) collective-permute-start(f32[8,8]{1,0:T(8,128)S(1)} %bitcast.47), channel_id=1, source_target_pairs={{0,1},{1,0},{2,3},{3,2},{4,5},{5,4},{6,7},{7,6},{8,9},{9,8},{10,11... | collective-permute-start | bytes 776 | tf_op jit(solution)/shard_map/ppermute | solution.py:101

commit v2 on v1

v2 whole, which is shorter than its diff:
```python
import math

import jax
import jax.numpy as jnp
from jax import lax
from jax.sharding import PartitionSpec as P


NLAT_GRID = 768
LAT0 = 256
REGIONS = 4
NTYPES = 8
STEPS = 4


def exchange(value, axis, bit):
    size = lax.axis_size(axis)
    return lax.ppermute(value, axis, [(i, i ^ bit) for i in range(size)])


def butterfly(value, axis):
    bit = 1
    while bit < lax.axis_size(axis):
        value = value + exchange(value, axis, bit)
        bit *= 2
    return value


def turned(value, axis, index):
    levs = lax.axis_size("lev")
    unit = value.shape[axis] // levs
    result = value
    for part in range(1, levs):
        head = lax.slice_in_dim(value, part * unit, value.shape[axis], axis=axis)
        tail = lax.slice_in_dim(value, 0, part * unit, axis=axis)
        result = jnp.where(index == part, jnp.concatenate([head, tail], axis=axis), result)
    return result


def local(
    anomalies,
    error_now,
    error_prior,
    energy_coef,
    obs_anomalies,
    innovations,
    valid_counts,
    type_ids,
    error_inverse,
):
    lat_rows = error_now.shape[2]
    lat_total = lat_rows * lax.axis_size("lat")
    lev_total = error_now.shape[1] * lax.axis_size("lev")
    lon_count = error_now.shape[3]
    variables = anomalies.shape[0]
    members = anomalies.shape[2]
    slot_count, local_members, block_rows = obs_anomalies.shape
    levs = lax.axis_size("lev")
    lev_index = lax.axis_index("lev")
    targets = variables * REGIONS
    own_targets = targets // levs
    shifts = [[(i, (i + step) % levs) for i in range(levs)] for step in range(levs)]

    lev_index, first_lat, error_now = lax.optimization_barrier(
        (lev_index, lax.axis_index("lat") * lat_rows, error_now)
    )

    lat_index = first_lat + jnp.arange(lat_rows, dtype=jnp.int32)
    cosine = jnp.cos(
        -0.5 * math.pi + ((lat_index + LAT0).astype(jnp.float32) + 0.5) * math.pi / NLAT_GRID
    )
    gradient = (
        (error_now + error_prior) * cosine[None, None, :, None] * energy_coef[:, :, None, None]
    ).astype(jnp.bfloat16)
    folded = jnp.einsum("vlkji,vlji->vkj", anomalies, gradient, preferred_element_type=jnp.float32)
    region = lat_index * REGIONS // lat_total
    onehot = (region[None, :] == jnp.arange(REGIONS, dtype=jnp.int32)[:, None]).astype(jnp.float32)
    partial = jnp.einsum("vkj,rj->vrk", folded, onehot, precision=lax.Precision.HIGHEST)
    partial = partial.reshape(targets, members)
    partial = butterfly(partial, "lev")
    partial = turned(turned(partial, 0, lev_index), 1, lev_index)

    type_table = type_ids[:, None] == jnp.arange(NTYPES, dtype=jnp.int32)[None, :]
    inverse_var = jnp.sum(
        jnp.where(type_table, error_inverse[None, :], jnp.zeros((), jnp.float32)), axis=1
    )
    positions = jnp.arange(block_rows, dtype=jnp.int32)
    row_mask = (positions[None, :] < valid_counts[:, None]).astype(jnp.float32)
    scaling = innovations * inverse_var[:, None] * row_mask / math.sqrt(members - 1)
    per_block = jnp.sum(obs_anomalies.astype(jnp.float32) * scaling[:, None, :], axis=2)
    per_type = jnp.einsum(
        "bc,bk->ck", type_table.astype(jnp.float32), per_block, precision=lax.Precision.HIGHEST
    )
    per_type = jnp.pad(per_type, ((0, 0), (0, members - local_members)))

    unit = slot_count // STEPS
    summed = jnp.concatenate([partial, per_type], axis=0)
    length = None
    bit = 1
    while bit < lax.axis_size("lat"):
        if bit == 2:
            summed, valid_counts = lax.optimization_barrier((summed, valid_counts))
        if bit == 4:
            summed, near_obs = lax.optimization_barrier((summed, obs_anomalies))
            near_obs = jnp.maximum(near_obs, jnp.finfo(near_obs.dtype).min)
            near_obs = lax.optimization_barrier(near_obs)
        added = exchange(summed, "lat", bit)
        if bit == 2:
            place = jnp.arange(slot_count, dtype=jnp.int32)
            marks = (valid_counts > 0) & (place > 0) & (place % unit == 0)
            length = jnp.sum(marks.astype(jnp.int32))
            summed, added, length = lax.optimization_barrier((summed, added, length))
        summed = summed + added
        bit *= 2
    norm_scale = math.sqrt(lev_total * lat_total * lon_count / REGIONS)
    weights = (summed[:targets] / norm_scale).astype(jnp.bfloat16)
    per_type = summed[targets:, :local_members]

    def respond(obs, part):
        return jnp.einsum("bks,tk->bts", obs, part, preferred_element_type=jnp.float32)

    def total_of(part):
        return jnp.einsum(
            "tk,ck->tc", part.astype(jnp.float32), per_type, precision=lax.Precision.HIGHEST
        )

    far = range(1, levs)
    parts = [
        weights[step * own_targets : (step + 1) * own_targets, :local_members]
        for step in range(levs)
    ]
    totals = [total_of(part) for part in parts]

    def finish(blocks):
        def run(obs, scaling, parts, totals):
            sent = [
                lax.optimization_barrier(respond(obs[:blocks], parts[step]).astype(jnp.bfloat16))
                for step in far
            ]
            received = []
            total = totals[0]
            for step in far:
                total = total + lax.ppermute(totals[step], "lev", shifts[step])
                received.append(lax.ppermute(sent[step - 1], "lev", shifts[step]))
            response = lax.optimization_barrier(respond(obs[:blocks], parts[0]))
            for part in received:
                response = response + part.astype(jnp.float32)
            impact = response * scaling[:blocks, None, :]
            block_total = slot_count * lax.axis_size("lat")
            total = total / math.sqrt(block_total * block_rows / NTYPES)
            return jnp.pad(impact, ((0, slot_count - blocks), (0, 0), (0, 0))), total

        return run

    return lax.switch(
        length,
        [finish((i + 1) * unit) for i in range(STEPS)],
        near_obs,
        scaling,
        parts,
        totals,
    )


def solution(mesh):
    in_specs = (
        P(None, "lev", None, "lat", None),
        P(None, "lev", "lat", None),
        P(None, "lev", "lat", None),
        P(None, "lev"),
        P("lat", "lev", None),
        P("lat", None),
        P("lat"),
        P("lat"),
        P(),
    )
    out_specs = (P("lat", "lev", None), P("lev", None))

    return jax.shard_map(local, mesh=mesh, in_specs=in_specs, out_specs=out_specs, check_vma=False)
```

time: 40 us -> 34.8 us (0.87)
  waiting for transfers between devices: 15.7 us -> 7.58 us
  other arithmetic: 5.51 us -> 8.55 us
  matrix products: 6.75 us -> 4.58 us
  local copies, waits for them, and re-layouts: 0.26 us -> 1.58 us
  between operations: 0.74 us -> 1.42 us
    ppermute x2, waiting for transfers between devices: 8.24 us -> 2.72 us  [the longest x1 2.72 us: run(): total = total + lax.ppermute(totals[step], 'lev', shifts[step])]
    max x0 -> x1, other arithmetic: none -> 3.47 us  [local(): near_obs = jnp.maximum(near_obs, jnp.finfo(near_obs.dtype).min)]
    ppermute x5, waiting for transfers between devices: 7.49 us -> 4.86 us  [exchange(): return lax.ppermute(value, axis, [(i, i ^ bit) for i in range(size)])]
    dot_general x3 -> x4, matrix products: 5.73 us -> 3.57 us  [the longest x2 3.33 us: respond(): jnp.einsum('bks,tk->bts', obs, part, preferred_element_type=jnp.float32)]
    pad x0 -> x1, local copies, waits for them, and re-layouts: none -> 1.04 us  [run(): return (jnp.pad(impact, ((0, slot_count - blocks), (0, 0), (0, 0))), total)]
    mul x1, other arithmetic: 0.88 us -> 0.07 us  [run(): impact = response * scaling[:blocks, None, :]]
    reduce_sum x0 -> x1, other arithmetic: none -> 0.63 us  [local(): length = jnp.sum(marks.astype(jnp.int32))]
    unnamed x6 -> x8, local copies, waits for them, and re-layouts: 0.02 us -> 0.45 us
  transfers between devices with their start and end apart: 7 -> 7, of which waited for: 5 -> 4; matrix products, arithmetic and copies ran while one was open for 9% -> 26% of each run, Pallas kernels for 0% -> 0%
where the time goes in v2:
time: 34.8 us; the launch traced here: 34.5 us
  starting transfers between devices  10.8 us (31%)
  other arithmetic  8.55 us (25%)
  waiting for transfers between devices  7.58 us (22%)
  matrix products  4.58 us (13%)
  local copies, waits for them, and re-layouts  1.58 us (5%)
  between operations  1.42 us (4%)
    ppermute x5, starting transfers between devices, exchange(): return lax.ppermute(value, axis, [(i, i ^ bit) for i in range(size)])  8.7 us
    ppermute x5, waiting for transfers between devices, exchange(): return lax.ppermute(value, axis, [(i, i ^ bit) for i in range(size)])  4.86 us
    max x1, other arithmetic, local(): near_obs = jnp.maximum(near_obs, jnp.finfo(near_obs.dtype).min)  3.47 us
    dot_general x2, matrix products, respond(): jnp.einsum('bks,tk->bts', obs, part, preferred_element_type=jnp.float32)  3.33 us
    ppermute x1, waiting for transfers between devices, run(): total = total + lax.ppermute(totals[step], 'lev', shifts[step])  2.72 us
    ppermute x1, starting transfers between devices, run(): total = total + lax.ppermute(totals[step], 'lev', shifts[step])  1.1 us
    another operation x1, other arithmetic  1.08 us
    pad x1, local copies, waits for them, and re-layouts, run(): return (jnp.pad(impact, ((0, slot_count - blocks), (0, 0), (0, 0))), total)  1.04 us
  transfers between devices with their start and end apart: 7, of which 4 were waited for; matrix products, arithmetic and copies ran while one was open for 26% of the time, Pallas kernels for 0%

profile of v2, /device:TPU:0, one launch (start us, length us, event | category | flops | bytes accessed | tf_op | source)
XLA Modules:
  0.0 34.5 jit_solution(14395219738675083496)
XLA Ops:
  0.7 1.1 %fusion.31 = bf16[4,2,1536,1]{2,1,0,3:T(2,128)(2,1)S(1)} fusion(f32[4]{0:T(128)} %bitcast.62, f32[2]{0:T(128)S(1)} %add_cosine_fusion, f32[4,1,2,1536]{3,2,1,0:T(2,128)} %param.14, f32[4,1,2,1536]{3,2,1,0:T(2,128)} %param.15), kind=kLoop, calls=%fused_computation.44 | loop fusion | flops 49152 | bytes 122904 | tf_op jit(solution)/shard_map/reshape.3
  1.8 0.4 %copy-done = bf16[4,1,80,2,1536]{4,3,2,1,0:T(2,128)(2,1)S(1)} copy-done((bf16[4,1,80,2,1536]{4,3,2,1,0:T(2,128)(2,1)S(1)}, bf16[4,1,80,2,1536]{4,3,2,1,0:T(2,128)(2,1)}, u32[]{:S(2)}) %copy-start) | copy-done | bytes 1966104
  2.2 0.6 %fusion.28 = f32[4,2,1,80]{3,2,1,0:T(1,128)S(1)} fusion(bf16[4,80,2,1536]{3,2,1,0:T(2,128)(2,1)S(1)} %bitcast.59, bf16[4,2,1536,1]{2,1,0,3:T(2,128)(2,1)S(1)} %fusion.31), kind=kOutput, calls=%fused_computation.37 | convolution fusion | flops 1966080 | bytes 1993216 | tf_op jit(solution)/shard_map/vlkji,vlji->vkj/dot_general | solution.py:75
  2.9 0.3 fusion.39
  3.1 3.0 %collective-permute-start.8 = (f32[16,80]{1,0:T(8,128)S(1)}, f32[16,80]{1,0:T(8,128)S(1)}, u32[]{:S(2)}, u32[]{:S(2)}) collective-permute-start(f32[16,80]{1,0:T(8,128)S(1)} %bitcast.60), channel_id=1, source_target_pairs={{0,1},{1,0},{2,3},{3,2},{4,5},{5,4},{6,7},{7,6},{8,9},{9,8},{10,11... | collective-permute-start | bytes 15368 | tf_op jit(solution)/shard_map/ppermute | solution.py:18
  6.1 0.8 %select_reduce_fusion = f32[128]{0:T(128)S(1)} fusion(f32[8]{0:T(128)} %param.21, s32[128]{0:T(128)} %param.20), kind=kLoop, calls=%fused_computation.51 | loop fusion | flops 2944 | bytes 1056 | tf_op jit(solution)/shard_map/reduce_sum | solution.py:84
  6.9 1.0 %select_multiply_fusion = f32[128,256]{1,0:T(8,128)S(1)} fusion(f32[128,256]{1,0:T(8,128)} %param.18, f32[128]{0:T(128)S(1)} %select_reduce_fusion, s32[128]{0:T(128)} %param.19), kind=kLoop, calls=%fused_computation.40 | loop fusion | flops 131072 | bytes 263168 | tf_op jit(solution)/shard_map/div | solution.py:89
  7.9 0.8 %multiply_reduce_fusion = f32[128,40]{1,0:T(8,128)S(1)} fusion(bf16[128,40,256]{2,1,0:T(8,128)(2,1)S(1)} %copy-done.2, f32[128,256]{1,0:T(8,128)S(1)} %select_multiply_fusion), kind=kLoop, calls=%fused_computation.36 | loop fusion | flops 3927040 | bytes 2772992 | tf_op jit(solution)/shard_map/reduce_sum | solution.py:90
  9.1 1.2 %collective-permute-done.9 = f32[24,80]{1,0:T(8,128)S(1)} collective-permute-done((f32[24,80]{1,0:T(8,128)S(1)}, f32[24,80]{1,0:T(8,128)S(1)}, u32[]{:S(2)}, u32[]{:S(2)}) %collective-permute-start.9) | collective-permute-done | bytes 7712 | tf_op jit(solution)/shard_map/ppermute | solution.py:18
  10.3 1.5 %collective-permute-start.10 = (f32[24,80]{1,0:T(8,128)S(1)}, f32[24,80]{1,0:T(8,128)S(1)}, u32[]{:S(2)}, u32[]{:S(2)}) collective-permute-start(f32[24,80]{1,0:T(8,128)S(1)} %fusion.47), channel_id=1, source_target_pairs={{0,4},{2,6},{4,0},{6,2},{8,12},{10,14},{12,8},{14,10},{16,20},{18,... | collective-permute-start | bytes 23048 | tf_op jit(solution)/shard_map/ppermute | solution.py:18
  11.7 0.6 %fusion.43 = s32[]{:T(128)} fusion(s32[128]{0:T(128)S(1)} %copy-done.4), kind=kLoop, calls=%fused_computation.69 | loop fusion | flops 1663 | bytes 516 | tf_op jit(solution)/shard_map/reduce_sum | solution.py:111
  12.4 1.6 %collective-permute-done.10 = f32[24,80]{1,0:T(8,128)S(1)} collective-permute-done((f32[24,80]{1,0:T(8,128)S(1)}, f32[24,80]{1,0:T(8,128)S(1)}, u32[]{:S(2)}, u32[]{:S(2)}) %collective-permute-start.10) | collective-permute-done | bytes 7712 | tf_op jit(solution)/shard_map/ppermute | solution.py:18
  14.0 1.6 %collective-permute-start.11 = (f32[24,80]{1,0:T(8,128)S(1)}, f32[24,80]{1,0:T(8,128)S(1)}, u32[]{:S(2)}, u32[]{:S(2)}) collective-permute-start(f32[24,80]{1,0:T(8,128)S(1)} %add.105), channel_id=1, source_target_pairs={{0,8},{2,10},{4,12},{6,14},{8,0},{10,2},{12,4},{14,6},{16,24},{18,... | collective-permute-start | bytes 23048 | tf_op jit(solution)/shard_map/ppermute | solution.py:18
  15.5 2.1 %collective-permute-done.11 = f32[24,80]{1,0:T(8,128)S(1)} collective-permute-done((f32[24,80]{1,0:T(8,128)S(1)}, f32[24,80]{1,0:T(8,128)S(1)}, u32[]{:S(2)}, u32[]{:S(2)}) %collective-permute-start.11) | collective-permute-done | bytes 7712 | tf_op jit(solution)/shard_map/ppermute | solution.py:18
  17.7 2.6 %collective-permute-start.12 = (f32[24,80]{1,0:T(8,128)S(1)}, f32[24,80]{1,0:T(8,128)S(1)}, u32[]{:S(2)}, u32[]{:S(2)}) collective-permute-start(f32[24,80]{1,0:T(8,128)S(1)} %add.106), channel_id=1, source_target_pairs={{0,16},{2,18},{4,20},{6,22},{8,24},{10,26},{12,28},{14,30},{16,0},... | collective-permute-start | bytes 23048 | tf_op jit(solution)/shard_map/ppermute | solution.py:18
  20.2 3.5 %broadcast_maximum_fusion = bf16[128,40,256]{2,1,0:T(8,128)(2,1)} fusion(bf16[128,40,256]{2,1,0:T(8,128)(2,1)} %param.17), kind=kLoop, calls=%fused_computation.39 | loop fusion | flops 1310720 | bytes 5242880 | tf_op jit(solution)/shard_map/max | solution.py:105
  24.6 9.9 %conditional.1 = (f32[128,8,256]{2,1,0:T(8,128)}, f32[8,8]{1,0:T(8,128)}) conditional(s32[]{:T(128)} %clamp.3, (bf16[128,40,256]{2,1,0:T(8,128)(2,1)}, bf16[8,40]{1,0:T(8,128)(2,1)S(1)}, bf16[8,40]{1,0:T(8,128)(2,1)S(1)}, f32[128,256]{1,0:T(8,128)S(1)}, f32[8,8]{1,0:T(8,128)S(1)}, ...), branch_computations={%region_3.4_spmd, %region_4.5_spmd, %region_5.6_spmd, %region_6.7_... | conditional | flops 42991744 | bytes 22154364 | solution.py:155
  24.6 1.7 %fusion.5 = bf16[64,8,256]{2,1,0:T(8,128)(2,1)S(1)} fusion(bf16[128,40,256]{2,1,0:T(8,128)(2,1)} %get-tuple-element.55, bf16[8,40]{1,0:T(8,128)(2,1)S(1)} %get-tuple-element.56), kind=kOutput, calls=%fused_computation.11 | convolution fusion | flops 10616832 | bytes 1573504 | tf_op jit(solution)/shard_map/cond/branch_1_fun/bks,tk->bts/dot_general | solution.py:120
  26.3 1.0 %collective-permute-start.2 = (bf16[64,8,256]{2,1,0:T(8,128)(2,1)S(1)}, bf16[64,8,256]{2,1,0:T(8,128)(2,1)S(1)}, u32[]{:S(2)}, u32[]{:S(2)}) collective-permute-start(bf16[64,8,256]{2,1,0:T(8,128)(2,1)S(1)} %fusion.5), channel_id=1, source_target_pairs={{0,1},{1,0},{2,3},{3,2},{4,5},{5,4},{6,7},{7,6},{8,9},{9,8},{10,11... | collective-permute-start | bytes 786440 | tf_op jit(solution)/shard_map/cond/branch_1_fun/ppermute | solution.py:144
  27.3 1.1 %collective-permute-start.3 = (f32[8,8]{1,0:T(8,128)S(1)}, f32[8,8]{1,0:T(8,128)S(1)}, u32[]{:S(2)}, u32[]{:S(2)}) collective-permute-start(f32[8,8]{1,0:T(8,128)S(1)} %get-tuple-element.59), channel_id=1, source_target_pairs={{0,1},{1,0},{2,3},{3,2},{4,5},{5,4},{6,7},{7,6},{8,9},{9,8},{10,11... | collective-permute-start | bytes 776 | tf_op jit(solution)/shard_map/cond/branch_1_fun/ppermute | solution.py:143
  28.4 1.7 %convolution_bitcast_fusion.1 = f32[64,8,256]{2,1,0:T(8,128)S(1)} fusion(bf16[128,40,256]{2,1,0:T(8,128)(2,1)} %get-tuple-element.55, bf16[8,40]{1,0:T(8,128)(2,1)S(1)} %get-tuple-element.54), kind=kOutput, calls=%fused_computation.9 | convolution fusion | flops 10485760 | bytes 1835648 | tf_op jit(solution)/shard_map/cond/branch_1_fun/bks,tk->bts/dot_general | solution.py:120
  30.1 2.7 %collective-permute-done.3 = f32[8,8]{1,0:T(8,128)S(1)} collective-permute-done((f32[8,8]{1,0:T(8,128)S(1)}, f32[8,8]{1,0:T(8,128)S(1)}, u32[]{:S(2)}, u32[]{:S(2)}) %collective-permute-start.3) | collective-permute-done | bytes 288 | tf_op jit(solution)/shard_map/cond/branch_1_fun/ppermute | solution.py:143
  32.8 0.6 %add_multiply_fusion.3 = f32[8,8]{1,0:T(8,128)} fusion(f32[8,8]{1,0:T(8,128)S(1)} %get-tuple-element.58, f32[8,8]{1,0:T(8,128)S(1)} %collective-permute-done.3), kind=kLoop, calls=%fused_computation.15 | loop fusion | flops 128 | bytes 768 | tf_op jit(solution)/shard_map/cond/branch_1_fun/div | solution.py:150
  33.5 1.0 %pad.13 = f32[128,8,256]{2,1,0:T(8,128)} pad(f32[64,8,256]{2,1,0:T(8,128)S(1)} %add_multiply_fusion.2, f32[]{:T(128)} %constant.67.clone), padding=0_64x0_0x0_0 | pad | bytes 1572868 | tf_op jit(solution)/shard_map/cond/branch_1_fun/jit(_pad)/pad | solution.py:151
  (30 shorter events, 0.8 us)
Async XLA Ops:
  0.6 1.6 %copy-start = (bf16[4,1,80,2,1536]{4,3,2,1,0:T(2,128)(2,1)S(1)}, bf16[4,1,80,2,1536]{4,3,2,1,0:T(2,128)(2,1)}, u32[]{:S(2)}) copy-start(bf16[4,1,80,2,1536]{4,3,2,1,0:T(2,128)(2,1)} %param.13) | copy-start | bytes 5898244
  0.7 7.3 %copy-start.2 = (bf16[128,40,256]{2,1,0:T(8,128)(2,1)S(1)}, bf16[128,40,256]{2,1,0:T(8,128)(2,1)}, u32[]{:S(2)}) copy-start(bf16[128,40,256]{2,1,0:T(8,128)(2,1)} %param.17) | copy-start | bytes 7864324
  2.2 6.4 %copy-start.3 = (s32[128]{0:T(128)S(1)}, s32[128]{0:T(128)}, u32[]{:S(2)}) copy-start(s32[128]{0:T(128)} %param.20) | copy-start | bytes 1540
  2.2 9.5 %copy-start.4 = (s32[128]{0:T(128)S(1)}, s32[128]{0:T(128)}, u32[]{:S(2)}) copy-start(s32[128]{0:T(128)} %param.19) | copy-start | bytes 1540
  3.1 5.7 %collective-permute-start.8 = (f32[16,80]{1,0:T(8,128)S(1)}, f32[16,80]{1,0:T(8,128)S(1)}, u32[]{:S(2)}, u32[]{:S(2)}) collective-permute-start(f32[16,80]{1,0:T(8,128)S(1)} %bitcast.60), channel_id=1, source_target_pairs={{0,1},{1,0},{2,3},{3,2},{4,5},{5,4},{6,7},{7,6},{8,9},{9,8},{10,11... | collective-permute-start | bytes 15368 | tf_op jit(solution)/shard_map/ppermute | solution.py:18
  9.0 1.2 %collective-permute-start.9 = (f32[24,80]{1,0:T(8,128)S(1)}, f32[24,80]{1,0:T(8,128)S(1)}, u32[]{:S(2)}, u32[]{:S(2)}) collective-permute-start(f32[24,80]{1,0:T(8,128)S(1)} %select_maximum_fusion), channel_id=1, source_target_pairs={{0,2},{2,0},{4,6},{6,4},{8,10},{10,8},{12,14},{14,12},{16,18},{18,... | collective-permute-start | bytes 23048 | tf_op jit(solution)/shard_map/ppermute | solution.py:18
  10.3 3.7 %collective-permute-start.10 = (f32[24,80]{1,0:T(8,128)S(1)}, f32[24,80]{1,0:T(8,128)S(1)}, u32[]{:S(2)}, u32[]{:S(2)}) collective-permute-start(f32[24,80]{1,0:T(8,128)S(1)} %fusion.47), channel_id=1, source_target_pairs={{0,4},{2,6},{4,0},{6,2},{8,12},{10,14},{12,8},{14,10},{16,20},{18,... | collective-permute-start | bytes 23048 | tf_op jit(solution)/shard_map/ppermute | solution.py:18
  14.0 3.7 %collective-permute-start.11 = (f32[24,80]{1,0:T(8,128)S(1)}, f32[24,80]{1,0:T(8,128)S(1)}, u32[]{:S(2)}, u32[]{:S(2)}) collective-permute-start(f32[24,80]{1,0:T(8,128)S(1)} %add.105), channel_id=1, source_target_pairs={{0,8},{2,10},{4,12},{6,14},{8,0},{10,2},{12,4},{14,6},{16,24},{18,... | collective-permute-start | bytes 23048 | tf_op jit(solution)/shard_map/ppermute | solution.py:18
  17.7 6.7 %collective-permute-start.12 = (f32[24,80]{1,0:T(8,128)S(1)}, f32[24,80]{1,0:T(8,128)S(1)}, u32[]{:S(2)}, u32[]{:S(2)}) collective-permute-start(f32[24,80]{1,0:T(8,128)S(1)} %add.106), channel_id=1, source_target_pairs={{0,16},{2,18},{4,20},{6,22},{8,24},{10,26},{12,28},{14,30},{16,0},... | collective-permute-start | bytes 23048 | tf_op jit(solution)/shard_map/ppermute | solution.py:18
  26.3 7.1 %collective-permute-start.2 = (bf16[64,8,256]{2,1,0:T(8,128)(2,1)S(1)}, bf16[64,8,256]{2,1,0:T(8,128)(2,1)S(1)}, u32[]{:S(2)}, u32[]{:S(2)}) collective-permute-start(bf16[64,8,256]{2,1,0:T(8,128)(2,1)S(1)} %fusion.5), channel_id=1, source_target_pairs={{0,1},{1,0},{2,3},{3,2},{4,5},{5,4},{6,7},{7,6},{8,9},{9,8},{10,11... | collective-permute-start | bytes 786440 | tf_op jit(solution)/shard_map/cond/branch_1_fun/ppermute | solution.py:144
  27.3 5.5 %collective-permute-start.3 = (f32[8,8]{1,0:T(8,128)S(1)}, f32[8,8]{1,0:T(8,128)S(1)}, u32[]{:S(2)}, u32[]{:S(2)}) collective-permute-start(f32[8,8]{1,0:T(8,128)S(1)} %get-tuple-element.59), channel_id=1, source_target_pairs={{0,1},{1,0},{2,3},{3,2},{4,5},{5,4},{6,7},{7,6},{8,9},{9,8},{10,11... | collective-permute-start | bytes 776 | tf_op jit(solution)/shard_map/cond/branch_1_fun/ppermute | solution.py:143

commit v3 on v2

--- a/solution.py
+++ b/solution.py
@@ -10,7 +10,8 @@
 LAT0 = 256
 REGIONS = 4
 NTYPES = 8
-STEPS = 4
+EARLY = (7, 32)
+STEPS = 10
 
 
 def exchange(value, axis, bit):
@@ -80,6 +81,13 @@
     partial = butterfly(partial, "lev")
     partial = turned(turned(partial, 0, lev_index), 1, lev_index)
 
+    unit = (slot_count - slot_count * EARLY[0] // EARLY[1]) // STEPS
+    early = slot_count - STEPS * unit
+    first_obs = lax.optimization_barrier(obs_anomalies[:early])
+    early_obs = []
+    for step in range(1, levs):
+        early_obs.append(lax.ppermute(first_obs, "lev", shifts[step]))
+
     type_table = type_ids[:, None] == jnp.arange(NTYPES, dtype=jnp.int32)[None, :]
     inverse_var = jnp.sum(
         jnp.where(type_table, error_inverse[None, :], jnp.zeros((), jnp.float32)), axis=1
@@ -93,25 +101,23 @@
     )
     per_type = jnp.pad(per_type, ((0, 0), (0, members - local_members)))
 
-    unit = slot_count // STEPS
+    place = jnp.arange(slot_count, dtype=jnp.int32)
+    marks = (valid_counts > 0) & (place >= early) & ((place - early) % unit == 0)
+    length = jnp.sum(marks.astype(jnp.int32))
     summed = jnp.concatenate([partial, per_type], axis=0)
-    length = None
     bit = 1
     while bit < lax.axis_size("lat"):
-        if bit == 2:
-            summed, valid_counts = lax.optimization_barrier((summed, valid_counts))
         if bit == 4:
             summed, near_obs = lax.optimization_barrier((summed, obs_anomalies))
             near_obs = jnp.maximum(near_obs, jnp.finfo(near_obs.dtype).min)
             near_obs = lax.optimization_barrier(near_obs)
-        added = exchange(summed, "lat", bit)
-        if bit == 2:
-            place = jnp.arange(slot_count, dtype=jnp.int32)
-            marks = (valid_counts > 0) & (place > 0) & (place % unit == 0)
-            length = jnp.sum(marks.astype(jnp.int32))
-            summed, added, length = lax.optimization_barrier((summed, added, length))
-        summed = summed + added
-        bit *= 2
+        if bit in (1,) and 4 * bit <= lax.axis_size("lat"):
+            added = [exchange(summed, "lat", bit * i) for i in (1, 2, 3)]
+            summed = (summed + added[0]) + (added[1] + added[2])
+            bit *= 4
+        else:
+            summed = summed + exchange(summed, "lat", bit)
+            bit *= 2
     norm_scale = math.sqrt(lev_total * lat_total * lon_count / REGIONS)
     weights = (summed[:targets] / norm_scale).astype(jnp.bfloat16)
     per_type = summed[targets:, :local_members]
@@ -131,20 +137,38 @@
     ]
     totals = [total_of(part) for part in parts]
 
-    def finish(blocks):
-        def run(obs, scaling, parts, totals):
-            sent = [
-                lax.optimization_barrier(respond(obs[:blocks], parts[step]).astype(jnp.bfloat16))
-                for step in far
-            ]
+    early_parts = []
+    for step in far:
+        low = (levs - step) * local_members
+        early_parts.append(weights[:own_targets, low : low + local_members])
+
+    def finish(late):
+        blocks = early + late
+
+        def run(obs, early_obs, scaling, parts, early_parts, totals):
+            total = totals[0]
             received = []
-            total = totals[0]
             for step in far:
-                total = total + lax.ppermute(totals[step], "lev", shifts[step])
-                received.append(lax.ppermute(sent[step - 1], "lev", shifts[step]))
-            response = lax.optimization_barrier(respond(obs[:blocks], parts[0]))
-            for part in received:
-                response = response + part.astype(jnp.float32)
+                moved = lax.ppermute(totals[step], "lev", shifts[step])
+                total = total + moved
+                if late:
+                    pieces = []
+                    for low, high in ((early, blocks - unit), (blocks - unit, blocks)):
+                        if low < high:
+                            sent = respond(obs[low:high], parts[step]).astype(jnp.bfloat16)
+                            sent = lax.optimization_barrier(sent)
+                            pieces.append(lax.ppermute(sent, "lev", shifts[step]))
+                    received.append(jnp.concatenate(pieces, axis=0))
+            own = lax.optimization_barrier(respond(obs[:blocks], parts[0]))
+            first = own[:early]
+            for step in far:
+                first = first + respond(early_obs[step - 1], early_parts[step - 1])
+            response = lax.optimization_barrier(first)
+            if late:
+                rest = own[early:]
+                for part in received:
+                    rest = rest + part.astype(jnp.float32)
+                response = jnp.concatenate([response, rest], axis=0)
             impact = response * scaling[:blocks, None, :]
             block_total = slot_count * lax.axis_size("lat")
             total = total / math.sqrt(block_total * block_rows / NTYPES)
@@ -154,10 +178,12 @@
 
     return lax.switch(
         length,
-        [finish((i + 1) * unit) for i in range(STEPS)],
+        [finish(i * unit) for i in range(STEPS + 1)],
         near_obs,
+        early_obs,
         scaling,
         parts,
+        early_parts,
         totals,
     )
 

time: 34.8 us -> 35.3 us (1.014)
  matrix products: 4.58 us -> 2.04 us
  starting transfers between devices: 10.8 us -> 13.1 us
  other arithmetic: 8.55 us -> 7.06 us
  local copies, waits for them, and re-layouts: 1.58 us -> 2.75 us
  waiting for transfers between devices: 7.58 us -> 8.7 us
    ppermute x2 -> x4, waiting for transfers between devices: 2.72 us -> 7.11 us  [the longest x1 4.94 us: local(): early_obs.append(lax.ppermute(first_obs, 'lev', shifts[step]))]
    ppermute x5 -> x6, waiting for transfers between devices: 4.86 us -> 1.59 us  [exchange(): return lax.ppermute(value, axis, [(i, i ^ bit) for i in range(size)])]
    dot_general x2 -> x4, matrix products: 3.33 us -> 0.79 us  [respond(): jnp.einsum('bks,tk->bts', obs, part, preferred_element_type=jnp.float32)]
    ppermute x2 -> x4, starting transfers between devices: 2.09 us -> 4.06 us  [the longest x2 2.14 us: run(): pieces.append(lax.ppermute(sent, 'lev', shifts[step]))]
    max x1, other arithmetic: 3.47 us -> 1.97 us  [local(): near_obs = jnp.maximum(near_obs, jnp.finfo(near_obs.dtype).min)]
    slice x0 -> x1, local copies, waits for them, and re-layouts: none -> 1.1 us  [local(): first_obs = lax.optimization_barrier(obs_anomalies[:early])]
    ppermute x5 -> x6, starting transfers between devices: 8.7 us -> 9.05 us  [exchange(): return lax.ppermute(value, axis, [(i, i ^ bit) for i in range(size)])]
  transfers between devices with their start and end apart: 7 -> 10, of which waited for: 4 -> 4; matrix products, arithmetic and copies ran while one was open for 26% -> 23% of each run, Pallas kernels for 0% -> 0%
where the time goes in v3:
time: 35.3 us; the launch traced here: 35.1 us
  starting transfers between devices  13.1 us (37%)
  waiting for transfers between devices  8.7 us (25%)
  other arithmetic  7.06 us (20%)
  local copies, waits for them, and re-layouts  2.75 us (8%)
  matrix products  2.04 us (6%)
  between operations  1.41 us (4%)
    ppermute x6, starting transfers between devices, exchange(): return lax.ppermute(value, axis, [(i, i ^ bit) for i in range(size)])  9.05 us
    ppermute x1, waiting for transfers between devices, local(): early_obs.append(lax.ppermute(first_obs, 'lev', shifts[step]))  4.94 us
    ppermute x1, waiting for transfers between devices, run(): moved = lax.ppermute(totals[step], 'lev', shifts[step])  2.16 us
    ppermute x2, starting transfers between devices, run(): pieces.append(lax.ppermute(sent, 'lev', shifts[step]))  2.14 us
    max x1, other arithmetic, local(): near_obs = jnp.maximum(near_obs, jnp.finfo(near_obs.dtype).min)  1.97 us
    ppermute x6, waiting for transfers between devices, exchange(): return lax.ppermute(value, axis, [(i, i ^ bit) for i in range(size)])  1.59 us
    slice x1, local copies, waits for them, and re-layouts, local(): first_obs = lax.optimization_barrier(obs_anomalies[:early])  1.1 us
    another operation x1, other arithmetic  1.08 us
  transfers between devices with their start and end apart: 10, of which 4 were waited for; matrix products, arithmetic and copies ran while one was open for 23% of the time, Pallas kernels for 0%

profile of v3, /device:TPU:0, one launch (start us, length us, event | category | flops | bytes accessed | tf_op | source)
XLA Modules:
  0.0 35.1 jit_solution(12406148147994174581)
XLA Ops:
  0.7 1.1 %fusion.151 = bf16[4,2,1536,1]{2,1,0,3:T(2,128)(2,1)S(1)} fusion(f32[4]{0:T(128)} %bitcast.250, f32[2]{0:T(128)S(1)} %add_cosine_fusion, f32[4,1,2,1536]{3,2,1,0:T(2,128)} %param.21, f32[4,1,2,1536]{3,2,1,0:T(2,128)} %param.22), kind=kLoop, calls=%fused_computation.191 | loop fusion | flops 49152 | bytes 122904 | tf_op jit(solution)/shard_map/reshape.3
  1.8 0.4 %copy-done = bf16[4,1,80,2,1536]{4,3,2,1,0:T(2,128)(2,1)S(1)} copy-done((bf16[4,1,80,2,1536]{4,3,2,1,0:T(2,128)(2,1)S(1)}, bf16[4,1,80,2,1536]{4,3,2,1,0:T(2,128)(2,1)}, u32[]{:S(2)}) %copy-start) | copy-done | bytes 1966104
  2.2 0.6 %fusion.148 = f32[4,2,1,80]{3,2,1,0:T(1,128)S(1)} fusion(bf16[4,80,2,1536]{3,2,1,0:T(2,128)(2,1)S(1)} %bitcast.247, bf16[4,2,1536,1]{2,1,0,3:T(2,128)(2,1)S(1)} %fusion.151), kind=kOutput, calls=%fused_computation.184 | convolution fusion | flops 1966080 | bytes 1993216 | tf_op jit(solution)/shard_map/vlkji,vlji->vkj/dot_general | solution.py:76
  3.1 3.0 %collective-permute-start.30 = (f32[16,80]{1,0:T(8,128)S(1)}, f32[16,80]{1,0:T(8,128)S(1)}, u32[]{:S(2)}, u32[]{:S(2)}) collective-permute-start(f32[16,80]{1,0:T(8,128)S(1)} %bitcast.248), channel_id=1, source_target_pairs={{0,1},{1,0},{2,3},{3,2},{4,5},{5,4},{6,7},{7,6},{8,9},{9,8},{10,11... | collective-permute-start | bytes 15368 | tf_op jit(solution)/shard_map/ppermute | solution.py:19
  6.1 0.8 %select_reduce_fusion = f32[128]{0:T(128)S(1)} fusion(f32[8]{0:T(128)} %param.28, s32[128]{0:T(128)} %param.27), kind=kLoop, calls=%fused_computation.199 | loop fusion | flops 2944 | bytes 1056 | tf_op jit(solution)/shard_map/reduce_sum | solution.py:92
  6.9 1.0 %select_multiply_fusion = f32[128,256]{1,0:T(8,128)S(1)} fusion(f32[128,256]{1,0:T(8,128)} %param.25, f32[128]{0:T(128)S(1)} %select_reduce_fusion, s32[128]{0:T(128)} %param.26), kind=kLoop, calls=%fused_computation.187 | loop fusion | flops 131072 | bytes 263168 | tf_op jit(solution)/shard_map/div | solution.py:97
  7.9 0.8 %multiply_reduce_fusion = f32[128,40]{1,0:T(8,128)S(1)} fusion(bf16[128,40,256]{2,1,0:T(8,128)(2,1)S(1)} %copy-done.1, f32[128,256]{1,0:T(8,128)S(1)} %select_multiply_fusion), kind=kLoop, calls=%fused_computation.183 | loop fusion | flops 3927040 | bytes 2772992 | tf_op jit(solution)/shard_map/reduce_sum | solution.py:98
  9.1 1.6 %collective-permute-start.32 = (f32[24,80]{1,0:T(8,128)S(1)}, f32[24,80]{1,0:T(8,128)S(1)}, u32[]{:S(2)}, u32[]{:S(2)}) collective-permute-start(f32[24,80]{1,0:T(8,128)S(1)} %select_maximum_fusion), channel_id=1, source_target_pairs={{0,4},{2,6},{4,0},{6,2},{8,12},{10,14},{12,8},{14,10},{16,20},{18,... | collective-permute-start | bytes 23048 | tf_op jit(solution)/shard_map/ppermute | solution.py:19
  10.9 1.1 %slice.214 = bf16[28,40,256]{2,1,0:T(8,128)(2,1)S(1)} slice(bf16[128,40,256]{2,1,0:T(8,128)(2,1)} %param.24), slice={[0:28], [0:40], [0:256]} | slice | bytes 1146880 | tf_op jit(solution)/shard_map/slice | solution.py:86
  12.0 1.0 %collective-permute-start.36 = (bf16[28,40,256]{2,1,0:T(8,128)(2,1)S(1)}, bf16[28,40,256]{2,1,0:T(8,128)(2,1)S(1)}, u32[]{:S(2)}, u32[]{:S(2)}) collective-permute-start(bf16[28,40,256]{2,1,0:T(8,128)(2,1)S(1)} %slice.214), channel_id=1, source_target_pairs={{0,1},{1,0},{2,3},{3,2},{4,5},{5,4},{6,7},{7,6},{8,9},{9,8},{10,11... | collective-permute-start | bytes 1720328 | tf_op jit(solution)/shard_map/ppermute | solution.py:89
  13.0 0.7 %collective-permute-done.33 = f32[24,80]{1,0:T(8,128)S(1)} collective-permute-done((f32[24,80]{1,0:T(8,128)S(1)}, f32[24,80]{1,0:T(8,128)S(1)}, u32[]{:S(2)}, u32[]{:S(2)}) %collective-permute-start.33) | collective-permute-done | bytes 7712 | tf_op jit(solution)/shard_map/ppermute | solution.py:19
  13.8 1.6 %collective-permute-start.34 = (f32[24,80]{1,0:T(8,128)S(1)}, f32[24,80]{1,0:T(8,128)S(1)}, u32[]{:S(2)}, u32[]{:S(2)}) collective-permute-start(f32[24,80]{1,0:T(8,128)S(1)} %add_add_fusion), channel_id=1, source_target_pairs={{0,8},{2,10},{4,12},{6,14},{8,0},{10,2},{12,4},{14,6},{16,24},{18,... | collective-permute-start | bytes 23048 | tf_op jit(solution)/shard_map/ppermute | solution.py:19
  15.3 0.6 %fusion.164 = s32[]{:T(128)} fusion(s32[128]{0:T(128)S(1)} %copy-done.3), kind=kLoop, calls=%fused_computation.220 | loop fusion | flops 1791 | bytes 516 | tf_op jit(solution)/shard_map/reduce_sum | solution.py:106
  16.6 0.8 %collective-permute-done.34 = f32[24,80]{1,0:T(8,128)S(1)} collective-permute-done((f32[24,80]{1,0:T(8,128)S(1)}, f32[24,80]{1,0:T(8,128)S(1)}, u32[]{:S(2)}, u32[]{:S(2)}) %collective-permute-start.34) | collective-permute-done | bytes 7712 | tf_op jit(solution)/shard_map/ppermute | solution.py:19
  17.5 2.6 %collective-permute-start.35 = (f32[24,80]{1,0:T(8,128)S(1)}, f32[24,80]{1,0:T(8,128)S(1)}, u32[]{:S(2)}, u32[]{:S(2)}) collective-permute-start(f32[24,80]{1,0:T(8,128)S(1)} %add.197), channel_id=1, source_target_pairs={{0,16},{2,18},{4,20},{6,22},{8,24},{10,26},{12,28},{14,30},{16,0},... | collective-permute-start | bytes 23048 | tf_op jit(solution)/shard_map/ppermute | solution.py:19
  20.1 2.0 %broadcast_maximum_fusion = bf16[128,40,256]{2,1,0:T(8,128)(2,1)S(1)} fusion(bf16[128,40,256]{2,1,0:T(8,128)(2,1)} %param.24), kind=kLoop, calls=%fused_computation.186 | loop fusion | flops 1310720 | bytes 5242880 | tf_op jit(solution)/shard_map/max | solution.py:112
  22.4 4.9 %collective-permute-done.36 = bf16[28,40,256]{2,1,0:T(8,128)(2,1)S(1)} collective-permute-done((bf16[28,40,256]{2,1,0:T(8,128)(2,1)S(1)}, bf16[28,40,256]{2,1,0:T(8,128)(2,1)S(1)}, u32[]{:S(2)}, u32[]{:S(2)}) %collective-permute-start.36) | collective-permute-done | bytes 573472 | tf_op jit(solution)/shard_map/ppermute | solution.py:89
  27.3 7.8 %conditional.1 = (f32[128,8,256]{2,1,0:T(8,128)}, f32[8,8]{1,0:T(8,128)}) conditional(s32[]{:T(128)} %clamp.3, (bf16[128,40,256]{2,1,0:T(8,128)(2,1)S(1)}, bf16[8,40]{1,0:T(8,128)(2,1)S(1)}, bf16[8,40]{1,0:T(8,128)(2,1)S(1)}, bf16[28,40,256]{2,1,0:T(8,128)(2,1)S(1)}, f32[128,256]{1,0:T(8,128)S(1)}, ...), branch_computations={%region_3.4_spmd, %region_4.5_spmd, %region_5.6_spmd, %region_6.7_... | conditional | flops 43344000 | bytes 14264844 | solution.py:179
  27.5 1.0 %collective-permute-start.3 = (bf16[10,8,256]{2,1,0:T(8,128)(2,1)S(1)}, bf16[10,8,256]{2,1,0:T(8,128)(2,1)S(1)}, u32[]{:S(2)}, u32[]{:S(2)}) collective-permute-start(bf16[10,8,256]{2,1,0:T(8,128)(2,1)S(1)} %fusion.12), channel_id=1, source_target_pairs={{0,1},{1,0},{2,3},{3,2},{4,5},{5,4},{6,7},{7,6},{8,9},{9,8},{10,11... | collective-permute-start | bytes 122888 | tf_op jit(solution)/shard_map/cond/branch_2_fun/ppermute | solution.py:160
  28.6 1.2 %collective-permute-start.4 = (bf16[10,8,256]{2,1,0:T(8,128)(2,1)S(1)}, bf16[10,8,256]{2,1,0:T(8,128)(2,1)S(1)}, u32[]{:S(2)}, u32[]{:S(2)}) collective-permute-start(bf16[10,8,256]{2,1,0:T(8,128)(2,1)S(1)} %fusion.13), channel_id=1, source_target_pairs={{0,1},{1,0},{2,3},{3,2},{4,5},{5,4},{6,7},{7,6},{8,9},{9,8},{10,11... | collective-permute-start | bytes 122888 | tf_op jit(solution)/shard_map/cond/branch_2_fun/ppermute | solution.py:160
  29.8 0.9 %collective-permute-start.5 = (f32[8,8]{1,0:T(8,128)S(1)}, f32[8,8]{1,0:T(8,128)S(1)}, u32[]{:S(2)}, u32[]{:S(2)}) collective-permute-start(f32[8,8]{1,0:T(8,128)S(1)} %get-tuple-element.196), channel_id=1, source_target_pairs={{0,1},{1,0},{2,3},{3,2},{4,5},{5,4},{6,7},{7,6},{8,9},{9,8},{10,11... | collective-permute-start | bytes 776 | tf_op jit(solution)/shard_map/cond/branch_2_fun/ppermute | solution.py:152
  31.2 2.2 %collective-permute-done.5 = f32[8,8]{1,0:T(8,128)S(1)} collective-permute-done((f32[8,8]{1,0:T(8,128)S(1)}, f32[8,8]{1,0:T(8,128)S(1)}, u32[]{:S(2)}, u32[]{:S(2)}) %collective-permute-start.5) | collective-permute-done | bytes 288 | tf_op jit(solution)/shard_map/cond/branch_2_fun/ppermute | solution.py:152
  33.4 0.6 %add_multiply_fusion.2 = f32[8,8]{1,0:T(8,128)} fusion(f32[8,8]{1,0:T(8,128)S(1)} %get-tuple-element.195, f32[8,8]{1,0:T(8,128)S(1)} %collective-permute-done.5), kind=kLoop, calls=%fused_computation.33 | loop fusion | flops 128 | bytes 768 | tf_op jit(solution)/shard_map/cond/branch_2_fun/div | solution.py:174
  34.1 1.0 %pad.35 = f32[128,8,256]{2,1,0:T(8,128)} pad(f32[48,8,256]{2,1,0:T(8,128)S(1)} %maximum_multiply_fusion.1, f32[]{:T(128)} %constant.96.clone), padding=0_80x0_0x0_0 | pad | bytes 1441796 | tf_op jit(solution)/shard_map/cond/branch_2_fun/jit(_pad)/pad | solution.py:175
  (39 shorter events, 2.2 us)
Async XLA Ops:
  0.6 1.6 %copy-start = (bf16[4,1,80,2,1536]{4,3,2,1,0:T(2,128)(2,1)S(1)}, bf16[4,1,80,2,1536]{4,3,2,1,0:T(2,128)(2,1)}, u32[]{:S(2)}) copy-start(bf16[4,1,80,2,1536]{4,3,2,1,0:T(2,128)(2,1)} %param.20) | copy-start | bytes 5898244
  0.7 7.2 %copy-start.1 = (bf16[128,40,256]{2,1,0:T(8,128)(2,1)S(1)}, bf16[128,40,256]{2,1,0:T(8,128)(2,1)}, u32[]{:S(2)}) copy-start(bf16[128,40,256]{2,1,0:T(8,128)(2,1)} %param.24) | copy-start | bytes 7864324
  2.2 6.4 %copy-start.2 = (s32[128]{0:T(128)S(1)}, s32[128]{0:T(128)}, u32[]{:S(2)}) copy-start(s32[128]{0:T(128)} %param.27) | copy-start | bytes 1540
  2.9 12.5 %copy-start.3 = (s32[128]{0:T(128)S(1)}, s32[128]{0:T(128)}, u32[]{:S(2)}) copy-start(s32[128]{0:T(128)} %param.26) | copy-start | bytes 1540
  3.1 5.7 %collective-permute-start.30 = (f32[16,80]{1,0:T(8,128)S(1)}, f32[16,80]{1,0:T(8,128)S(1)}, u32[]{:S(2)}, u32[]{:S(2)}) collective-permute-start(f32[16,80]{1,0:T(8,128)S(1)} %bitcast.248), channel_id=1, source_target_pairs={{0,1},{1,0},{2,3},{3,2},{4,5},{5,4},{6,7},{7,6},{8,9},{9,8},{10,11... | collective-permute-start | bytes 15368 | tf_op jit(solution)/shard_map/ppermute | solution.py:19
  9.0 4.0 %collective-permute-start.31 = (f32[24,80]{1,0:T(8,128)S(1)}, f32[24,80]{1,0:T(8,128)S(1)}, u32[]{:S(2)}, u32[]{:S(2)}) collective-permute-start(f32[24,80]{1,0:T(8,128)S(1)} %select_maximum_fusion), channel_id=1, source_target_pairs={{0,2},{2,0},{4,6},{6,4},{8,10},{10,8},{12,14},{14,12},{16,18},{18,... | collective-permute-start | bytes 23048 | tf_op jit(solution)/shard_map/ppermute | solution.py:19
  9.1 3.9 %collective-permute-start.32 = (f32[24,80]{1,0:T(8,128)S(1)}, f32[24,80]{1,0:T(8,128)S(1)}, u32[]{:S(2)}, u32[]{:S(2)}) collective-permute-start(f32[24,80]{1,0:T(8,128)S(1)} %select_maximum_fusion), channel_id=1, source_target_pairs={{0,4},{2,6},{4,0},{6,2},{8,12},{10,14},{12,8},{14,10},{16,20},{18,... | collective-permute-start | bytes 23048 | tf_op jit(solution)/shard_map/ppermute | solution.py:19
  10.6 3.1 %collective-permute-start.33 = (f32[24,80]{1,0:T(8,128)S(1)}, f32[24,80]{1,0:T(8,128)S(1)}, u32[]{:S(2)}, u32[]{:S(2)}) collective-permute-start(f32[24,80]{1,0:T(8,128)S(1)} %select_maximum_fusion), channel_id=1, source_target_pairs={{0,6},{2,4},{4,2},{6,0},{8,14},{10,12},{12,10},{14,8},{16,22},{18,... | collective-permute-start | bytes 23048 | tf_op jit(solution)/shard_map/ppermute | solution.py:19
  12.0 15.3 %collective-permute-start.36 = (bf16[28,40,256]{2,1,0:T(8,128)(2,1)S(1)}, bf16[28,40,256]{2,1,0:T(8,128)(2,1)S(1)}, u32[]{:S(2)}, u32[]{:S(2)}) collective-permute-start(bf16[28,40,256]{2,1,0:T(8,128)(2,1)S(1)} %slice.214), channel_id=1, source_target_pairs={{0,1},{1,0},{2,3},{3,2},{4,5},{5,4},{6,7},{7,6},{8,9},{9,8},{10,11... | collective-permute-start | bytes 1720328 | tf_op jit(solution)/shard_map/ppermute | solution.py:89
  13.8 3.7 %collective-permute-start.34 = (f32[24,80]{1,0:T(8,128)S(1)}, f32[24,80]{1,0:T(8,128)S(1)}, u32[]{:S(2)}, u32[]{:S(2)}) collective-permute-start(f32[24,80]{1,0:T(8,128)S(1)} %add_add_fusion), channel_id=1, source_target_pairs={{0,8},{2,10},{4,12},{6,14},{8,0},{10,2},{12,4},{14,6},{16,24},{18,... | collective-permute-start | bytes 23048 | tf_op jit(solution)/shard_map/ppermute | solution.py:19
  17.5 4.6 %collective-permute-start.35 = (f32[24,80]{1,0:T(8,128)S(1)}, f32[24,80]{1,0:T(8,128)S(1)}, u32[]{:S(2)}, u32[]{:S(2)}) collective-permute-start(f32[24,80]{1,0:T(8,128)S(1)} %add.197), channel_id=1, source_target_pairs={{0,16},{2,18},{4,20},{6,22},{8,24},{10,26},{12,28},{14,30},{16,0},... | collective-permute-start | bytes 23048 | tf_op jit(solution)/shard_map/ppermute | solution.py:19
  27.5 6.5 %collective-permute-start.3 = (bf16[10,8,256]{2,1,0:T(8,128)(2,1)S(1)}, bf16[10,8,256]{2,1,0:T(8,128)(2,1)S(1)}, u32[]{:S(2)}, u32[]{:S(2)}) collective-permute-start(bf16[10,8,256]{2,1,0:T(8,128)(2,1)S(1)} %fusion.12), channel_id=1, source_target_pairs={{0,1},{1,0},{2,3},{3,2},{4,5},{5,4},{6,7},{7,6},{8,9},{9,8},{10,11... | collective-permute-start | bytes 122888 | tf_op jit(solution)/shard_map/cond/branch_2_fun/ppermute | solution.py:160
  28.6 5.4 %collective-permute-start.4 = (bf16[10,8,256]{2,1,0:T(8,128)(2,1)S(1)}, bf16[10,8,256]{2,1,0:T(8,128)(2,1)S(1)}, u32[]{:S(2)}, u32[]{:S(2)}) collective-permute-start(bf16[10,8,256]{2,1,0:T(8,128)(2,1)S(1)} %fusion.13), channel_id=1, source_target_pairs={{0,1},{1,0},{2,3},{3,2},{4,5},{5,4},{6,7},{7,6},{8,9},{9,8},{10,11... | collective-permute-start | bytes 122888 | tf_op jit(solution)/shard_map/cond/branch_2_fun/ppermute | solution.py:160
  29.8 3.6 %collective-permute-start.5 = (f32[8,8]{1,0:T(8,128)S(1)}, f32[8,8]{1,0:T(8,128)S(1)}, u32[]{:S(2)}, u32[]{:S(2)}) collective-permute-start(f32[8,8]{1,0:T(8,128)S(1)} %get-tuple-element.196), channel_id=1, source_target_pairs={{0,1},{1,0},{2,3},{3,2},{4,5},{5,4},{6,7},{7,6},{8,9},{9,8},{10,11... | collective-permute-start | bytes 776 | tf_op jit(solution)/shard_map/cond/branch_2_fun/ppermute | solution.py:152

commit v4 on v3

--- a/solution.py
+++ b/solution.py
@@ -10,8 +10,8 @@
 LAT0 = 256
 REGIONS = 4
 NTYPES = 8
-EARLY = (7, 32)
-STEPS = 10
+EARLY = (4, 32)
+STEPS = 16
 
 
 def exchange(value, axis, bit):
@@ -73,10 +73,22 @@
     gradient = (
         (error_now + error_prior) * cosine[None, None, :, None] * energy_coef[:, :, None, None]
     ).astype(jnp.bfloat16)
-    folded = jnp.einsum("vlkji,vlji->vkj", anomalies, gradient, preferred_element_type=jnp.float32)
+    lat_index = first_lat + jnp.arange(lat_rows, dtype=jnp.int32)
     region = lat_index * REGIONS // lat_total
-    onehot = (region[None, :] == jnp.arange(REGIONS, dtype=jnp.int32)[:, None]).astype(jnp.float32)
-    partial = jnp.einsum("vkj,rj->vrk", folded, onehot, precision=lax.Precision.HIGHEST)
+    if lat_total % (REGIONS * lat_rows) == 0:
+        folded = jnp.einsum(
+            "vlkji,vlji->vk", anomalies, gradient, preferred_element_type=jnp.float32
+        )
+        mine = region[0] == jnp.arange(REGIONS, dtype=jnp.int32)
+        partial = jnp.where(mine[None, :, None], folded[:, None, :], jnp.zeros((), jnp.float32))
+    else:
+        folded = jnp.einsum(
+            "vlkji,vlji->vkj", anomalies, gradient, preferred_element_type=jnp.float32
+        )
+        onehot = region[None, :] == jnp.arange(REGIONS, dtype=jnp.int32)[:, None]
+        partial = jnp.einsum(
+            "vkj,rj->vrk", folded, onehot.astype(jnp.float32), precision=lax.Precision.HIGHEST
+        )
     partial = partial.reshape(targets, members)
     partial = butterfly(partial, "lev")
     partial = turned(turned(partial, 0, lev_index), 1, lev_index)
@@ -89,16 +101,28 @@
         early_obs.append(lax.ppermute(first_obs, "lev", shifts[step]))
 
     type_table = type_ids[:, None] == jnp.arange(NTYPES, dtype=jnp.int32)[None, :]
-    inverse_var = jnp.sum(
-        jnp.where(type_table, error_inverse[None, :], jnp.zeros((), jnp.float32)), axis=1
-    )
     positions = jnp.arange(block_rows, dtype=jnp.int32)
     row_mask = (positions[None, :] < valid_counts[:, None]).astype(jnp.float32)
-    scaling = innovations * inverse_var[:, None] * row_mask / math.sqrt(members - 1)
-    per_block = jnp.sum(obs_anomalies.astype(jnp.float32) * scaling[:, None, :], axis=2)
+    root = math.sqrt(members - 1)
+    per_block = jnp.sum(
+        obs_anomalies.astype(jnp.float32) * (innovations * row_mask)[:, None, :], axis=2
+    )
     per_type = jnp.einsum(
         "bc,bk->ck", type_table.astype(jnp.float32), per_block, precision=lax.Precision.HIGHEST
     )
+    per_type = per_type * error_inverse[:, None] / root
+
+    per_type, late_innovations, late_counts, late_types = lax.optimization_barrier(
+        (per_type, innovations, valid_counts, type_ids)
+    )
+    late_table = late_types[:, None] == jnp.arange(NTYPES, dtype=jnp.int32)[None, :]
+    inverse_var = jnp.sum(
+        jnp.where(late_table, error_inverse[None, :], jnp.zeros((), jnp.float32)), axis=1
+    )
+    inverse_var = lax.optimization_barrier(inverse_var)
+    late_mask = (positions[None, :] < late_counts[:, None]).astype(jnp.float32)
+    scaling = late_innovations * inverse_var[:, None] * late_mask / root
+    scaling = lax.optimization_barrier(scaling)
     per_type = jnp.pad(per_type, ((0, 0), (0, members - local_members)))
 
     place = jnp.arange(slot_count, dtype=jnp.int32)
@@ -125,7 +149,7 @@
     def respond(obs, part):
         return jnp.einsum("bks,tk->bts", obs, part, preferred_element_type=jnp.float32)
 
-    def total_of(part):
+    def total_of(part, per_type):
         return jnp.einsum(
             "tk,ck->tc", part.astype(jnp.float32), per_type, precision=lax.Precision.HIGHEST
         )
@@ -135,7 +159,6 @@
         weights[step * own_targets : (step + 1) * own_targets, :local_members]
         for step in range(levs)
     ]
-    totals = [total_of(part) for part in parts]
 
     early_parts = []
     for step in far:
@@ -144,8 +167,10 @@
 
     def finish(late):
         blocks = early + late
-
-        def run(obs, early_obs, scaling, parts, early_parts, totals):
+        middle = early + late // unit // 2 * unit
+
+        def run(obs, early_obs, scaling, parts, early_parts, per_type):
+            totals = [lax.optimization_barrier(total_of(part, per_type)) for part in parts]
             total = totals[0]
             received = []
             for step in far:
@@ -153,26 +178,39 @@
                 total = total + moved
                 if late:
                     pieces = []
-                    for low, high in ((early, blocks - unit), (blocks - unit, blocks)):
+                    for low, high in ((early, middle), (middle, blocks)):
                         if low < high:
                             sent = respond(obs[low:high], parts[step]).astype(jnp.bfloat16)
                             sent = lax.optimization_barrier(sent)
                             pieces.append(lax.ppermute(sent, "lev", shifts[step]))
-                    received.append(jnp.concatenate(pieces, axis=0))
+                    received.append(pieces)
             own = lax.optimization_barrier(respond(obs[:blocks], parts[0]))
             first = own[:early]
             for step in far:
                 first = first + respond(early_obs[step - 1], early_parts[step - 1])
             response = lax.optimization_barrier(first)
+
+            def scaled(response, low, high):
+                return response * scaling[low:high, None, :]
+
+            def arrived(piece, low, high):
+                rest = own[low:high]
+                for part in received:
+                    rest = rest + part[piece].astype(jnp.float32)
+                return rest
+
+            if middle > early:
+                response = jnp.concatenate([response, arrived(0, early, middle)], axis=0)
+            impact = jnp.pad(
+                scaled(response, 0, middle), ((0, slot_count - middle), (0, 0), (0, 0))
+            )
             if late:
-                rest = own[early:]
-                for part in received:
-                    rest = rest + part.astype(jnp.float32)
-                response = jnp.concatenate([response, rest], axis=0)
-            impact = response * scaling[:blocks, None, :]
+                impact = lax.optimization_barrier(impact)
+                rest = scaled(arrived(-1, middle, blocks), middle, blocks)
+                impact = lax.dynamic_update_slice(impact, rest, (middle, 0, 0))
             block_total = slot_count * lax.axis_size("lat")
             total = total / math.sqrt(block_total * block_rows / NTYPES)
-            return jnp.pad(impact, ((0, slot_count - blocks), (0, 0), (0, 0))), total
+            return impact, total
 
         return run
 
@@ -184,7 +222,7 @@
         scaling,
         parts,
         early_parts,
-        totals,
+        per_type,
     )
 
 

time: 35.3 us -> 34.6 us (0.980)
  the two profiles are of different devices: /device:TPU:0 before, /device:TPU:18 now
where the time goes in v4:
time: 34.6 us; the launch traced here: 34.4 us
  starting transfers between devices  9.57 us (28%)
  waiting for transfers between devices  7.08 us (20%)
  other arithmetic  5.78 us (17%)
  loops' own time  5.7 us (16%)
  local copies, waits for them, and re-layouts  2.59 us (7%)
  matrix products  2.06 us (6%)
  between operations  1.63 us (5%)
    another operation x1, loops' own time, local(): lax.switch(length, [finish(i * unit) for i in range(STEPS + 1)], near_obs...  5.7 us
    ppermute x6, starting transfers between devices, exchange(): return lax.ppermute(value, axis, [(i, i ^ bit) for i in range(size)])  5.31 us
    ppermute x6, waiting for transfers between devices, exchange(): return lax.ppermute(value, axis, [(i, i ^ bit) for i in range(size)])  5.09 us
    ppermute x2, starting transfers between devices, run(): pieces.append(lax.ppermute(sent, 'lev', shifts[step]))  2.16 us
    ppermute x1, waiting for transfers between devices, run(): moved = lax.ppermute(totals[step], 'lev', shifts[step])  1.97 us
    max x1, other arithmetic, local(): near_obs = jnp.maximum(near_obs, jnp.finfo(near_obs.dtype).min)  1.97 us
    ppermute x1, starting transfers between devices, run(): moved = lax.ppermute(totals[step], 'lev', shifts[step])  1.53 us
    another operation x1, other arithmetic  1.08 us
  transfers between devices with their start and end apart: 10, of which 4 were waited for; matrix products, arithmetic and copies ran while one was open for 20% of the time, Pallas kernels for 0%

profile of v4, /device:TPU:18, one launch (start us, length us, event | category | flops | bytes accessed | tf_op | source)
XLA Modules:
  0.0 34.4 jit_solution(13466632666386673490)
XLA Ops:
  0.9 1.1 %fusion.234 = bf16[4,2,1536,1]{2,1,0,3:T(2,128)(2,1)S(1)} fusion(f32[4]{0:T(128)} %bitcast.446, f32[2]{0:T(128)S(1)} %add_cosine_fusion, f32[4,1,2,1536]{3,2,1,0:T(2,128)} %param.27, f32[4,1,2,1536]{3,2,1,0:T(2,128)} %param.28), kind=kLoop, calls=%fused_computation.345 | loop fusion | flops 49152 | bytes 122904 | tf_op jit(solution)/shard_map/reshape.6
  2.0 0.3 copy-done
  2.2 0.6 %fusion.228 = f32[4,1,80,1]{2,1,3,0:T(1,128)S(1)} fusion(bf16[4,80,2,1536]{3,2,1,0:T(2,128)(2,1)S(1)} %bitcast.442, bf16[4,2,1536,1]{2,1,0,3:T(2,128)(2,1)S(1)} %fusion.234), kind=kOutput, calls=%fused_computation.332 | convolution fusion | flops 1966080 | bytes 1991936 | tf_op jit(solution)/shard_map/vlkji,vlji->vk/dot_general | solution.py:79
  2.9 1.5 %collective-permute-start.48 = (f32[16,80]{1,0:T(8,128)S(1)}, f32[16,80]{1,0:T(8,128)S(1)}, u32[]{:S(2)}, u32[]{:S(2)}) collective-permute-start(f32[16,80]{1,0:T(8,128)S(1)} %broadcast_select_fusion), channel_id=1, source_target_pairs={{0,1},{1,0},{2,3},{3,2},{4,5},{5,4},{6,7},{7,6},{8,9},{9,8},{10,11... | collective-permute-start | bytes 15368 | tf_op jit(solution)/shard_map/ppermute | solution.py:19
  4.5 1.0 %slice.422 = bf16[16,40,256]{2,1,0:T(8,128)(2,1)S(1)} slice(bf16[128,40,256]{2,1,0:T(8,128)(2,1)} %param.30), slice={[0:16], [0:40], [0:256]} | slice | bytes 655360 | tf_op jit(solution)/shard_map/slice | solution.py:98
  5.5 0.6 %collective-permute-start.54 = (bf16[16,40,256]{2,1,0:T(8,128)(2,1)S(1)}, bf16[16,40,256]{2,1,0:T(8,128)(2,1)S(1)}, u32[]{:S(2)}, u32[]{:S(2)}) collective-permute-start(bf16[16,40,256]{2,1,0:T(8,128)(2,1)S(1)} %slice.422), channel_id=1, source_target_pairs={{0,1},{1,0},{2,3},{3,2},{4,5},{5,4},{6,7},{7,6},{8,9},{9,8},{10,11... | collective-permute-start | bytes 983048 | tf_op jit(solution)/shard_map/ppermute | solution.py:101
  6.2 0.8 %multiply_reduce_fusion = f32[128,40]{1,0:T(8,128)S(1)} fusion(bf16[128,40,256]{2,1,0:T(8,128)(2,1)S(1)} %copy-done.1, f32[128,256]{1,0:T(8,128)S(1)} %fusion.231), kind=kLoop, calls=%fused_computation.331 | loop fusion | flops 3927040 | bytes 2772992 | tf_op jit(solution)/shard_map/reduce_sum | solution.py:107
  6.9 0.3 fusion.230
  7.6 0.6 %collective-permute-start.50 = (f32[24,80]{1,0:T(8,128)S(1)}, f32[24,80]{1,0:T(8,128)S(1)}, u32[]{:S(2)}, u32[]{:S(2)}) collective-permute-start(f32[24,80]{1,0:T(8,128)S(1)} %select_maximum_fusion), channel_id=1, source_target_pairs={{0,4},{2,6},{4,0},{6,2},{8,12},{10,14},{12,8},{14,10},{16,20},{18,... | collective-permute-start | bytes 23048 | tf_op jit(solution)/shard_map/ppermute | solution.py:19
  8.2 1.2 %collective-permute-start.51 = (f32[24,80]{1,0:T(8,128)S(1)}, f32[24,80]{1,0:T(8,128)S(1)}, u32[]{:S(2)}, u32[]{:S(2)}) collective-permute-start(f32[24,80]{1,0:T(8,128)S(1)} %select_maximum_fusion), channel_id=1, source_target_pairs={{0,6},{2,4},{4,2},{6,0},{8,14},{10,12},{12,10},{14,8},{16,22},{18,... | collective-permute-start | bytes 23048 | tf_op jit(solution)/shard_map/ppermute | solution.py:19
  9.6 1.9 %collective-permute-done.50 = f32[24,80]{1,0:T(8,128)S(1)} collective-permute-done((f32[24,80]{1,0:T(8,128)S(1)}, f32[24,80]{1,0:T(8,128)S(1)}, u32[]{:S(2)}, u32[]{:S(2)}) %collective-permute-start.50) | collective-permute-done | bytes 7712 | tf_op jit(solution)/shard_map/ppermute | solution.py:19
  11.5 1.6 %collective-permute-start.52 = (f32[24,80]{1,0:T(8,128)S(1)}, f32[24,80]{1,0:T(8,128)S(1)}, u32[]{:S(2)}, u32[]{:S(2)}) collective-permute-start(f32[24,80]{1,0:T(8,128)S(1)} %add_add_fusion), channel_id=1, source_target_pairs={{0,8},{2,10},{4,12},{6,14},{8,0},{10,2},{12,4},{14,6},{16,24},{18,... | collective-permute-start | bytes 23048 | tf_op jit(solution)/shard_map/ppermute | solution.py:19
  13.1 0.6 %fusion.236 = s32[]{:T(128)} fusion(s32[128]{0:T(128)S(1)} %copy-done.19), kind=kLoop, calls=%fused_computation.365 | loop fusion | flops 1791 | bytes 516 | tf_op jit(solution)/shard_map/reduce_sum | solution.py:130
  14.4 0.8 %collective-permute-done.52 = f32[24,80]{1,0:T(8,128)S(1)} collective-permute-done((f32[24,80]{1,0:T(8,128)S(1)}, f32[24,80]{1,0:T(8,128)S(1)}, u32[]{:S(2)}, u32[]{:S(2)}) %collective-permute-start.52) | collective-permute-done | bytes 7712 | tf_op jit(solution)/shard_map/ppermute | solution.py:19
  15.5 2.0 %broadcast_maximum_fusion = bf16[128,40,256]{2,1,0:T(8,128)(2,1)S(1)} fusion(bf16[128,40,256]{2,1,0:T(8,128)(2,1)} %param.30), kind=kLoop, calls=%fused_computation.334 | loop fusion | flops 1310720 | bytes 5242880 | tf_op jit(solution)/shard_map/max | solution.py:136
  17.5 2.4 %collective-permute-done.53 = f32[24,80]{1,0:T(8,128)S(1)} collective-permute-done((f32[24,80]{1,0:T(8,128)S(1)}, f32[24,80]{1,0:T(8,128)S(1)}, u32[]{:S(2)}, u32[]{:S(2)}) %collective-permute-start.53) | collective-permute-done | bytes 7712 | tf_op jit(solution)/shard_map/ppermute | solution.py:19
  19.9 14.3 %conditional.1 = (f32[128,8,256]{2,1,0:T(8,128)}, f32[8,8]{1,0:T(8,128)}) conditional(s32[]{:T(128)} %clamp.3, (bf16[128,40,256]{2,1,0:T(8,128)(2,1)S(1)}, bf16[8,40]{1,0:T(8,128)(2,1)S(1)}, bf16[8,40]{1,0:T(8,128)(2,1)S(1)}, bf16[16,40,256]{2,1,0:T(8,128)(2,1)S(1)}, f32[128,256]{1,0:T(8,128)S(1)}, ...), branch_computations={%region_3.4_spmd, %region_4.5_spmd, %region_5.6_spmd, %region_6.7_... | conditional | flops 43135104 | bytes 18558376 | solution.py:217
  20.1 1.6 %collective-permute-start.21 = (bf16[28,8,256]{2,1,0:T(8,128)(2,1)S(1)}, bf16[28,8,256]{2,1,0:T(8,128)(2,1)S(1)}, u32[]{:S(2)}, u32[]{:S(2)}) collective-permute-start(bf16[28,8,256]{2,1,0:T(8,128)(2,1)S(1)} %fusion.95), channel_id=1, source_target_pairs={{0,1},{1,0},{2,3},{3,2},{4,5},{5,4},{6,7},{7,6},{8,9},{9,8},{10,11... | collective-permute-start | bytes 344072 | tf_op jit(solution)/shard_map/cond/branch_8_fun/ppermute | solution.py:185
  21.9 0.6 %collective-permute-start.22 = (bf16[28,8,256]{2,1,0:T(8,128)(2,1)S(1)}, bf16[28,8,256]{2,1,0:T(8,128)(2,1)S(1)}, u32[]{:S(2)}, u32[]{:S(2)}) collective-permute-start(bf16[28,8,256]{2,1,0:T(8,128)(2,1)S(1)} %fusion.96), channel_id=1, source_target_pairs={{0,1},{1,0},{2,3},{3,2},{4,5},{5,4},{6,7},{7,6},{8,9},{9,8},{10,11... | collective-permute-start | bytes 344072 | tf_op jit(solution)/shard_map/cond/branch_8_fun/ppermute | solution.py:185
  22.6 1.5 %collective-permute-start.23 = (f32[8,8]{1,0:T(8,128)S(1)}, f32[8,8]{1,0:T(8,128)S(1)}, u32[]{:S(2)}, u32[]{:S(2)}) collective-permute-start(f32[8,8]{1,0:T(8,128)S(1)} %fusion.257), channel_id=1, source_target_pairs={{0,1},{1,0},{2,3},{3,2},{4,5},{5,4},{6,7},{7,6},{8,9},{9,8},{10,11... | collective-permute-start | bytes 776 | tf_op jit(solution)/shard_map/cond/branch_8_fun/ppermute | solution.py:177
  24.2 0.4 %fusion.91 = f32[72,8,256]{2,1,0:T(8,128)S(1)} fusion(bf16[128,40,256]{2,1,0:T(8,128)(2,1)S(1)} %get-tuple-element.295, bf16[8,40]{1,0:T(8,128)(2,1)S(1)} %get-tuple-element.294), kind=kOutput, calls=%fused_computation.146 | convolution fusion | flops 11796480 | bytes 2066432 | tf_op jit(solution)/shard_map/cond/branch_8_fun/bks,tk->bts/dot_general | solution.py:150
  24.9 2.0 %collective-permute-done.23 = f32[8,8]{1,0:T(8,128)S(1)} collective-permute-done((f32[8,8]{1,0:T(8,128)S(1)}, f32[8,8]{1,0:T(8,128)S(1)}, u32[]{:S(2)}, u32[]{:S(2)}) %collective-permute-start.23) | collective-permute-done | bytes 288 | tf_op jit(solution)/shard_map/cond/branch_8_fun/ppermute | solution.py:177
  26.8 0.6 %add_multiply_fusion.8 = f32[8,8]{1,0:T(8,128)} fusion(f32[8,8]{1,0:T(8,128)S(1)} %fusion.256, f32[8,8]{1,0:T(8,128)S(1)} %collective-permute-done.23), kind=kLoop, calls=%fused_computation.160 | loop fusion | flops 128 | bytes 768 | tf_op jit(solution)/shard_map/cond/branch_8_fun/div | solution.py:212
  27.7 1.0 %copy-done.9 = f32[128,8,256]{2,1,0:T(8,128)} copy-done((f32[128,8,256]{2,1,0:T(8,128)}, f32[128,8,256]{2,1,0:T(8,128)S(1)}, u32[]{:S(2)}) %copy-start.9) | copy-done | bytes 1048600 | tf_op jit(solution)/shard_map/cond
  (53 shorter events, 2.2 us)
Async XLA Ops:
  0.6 1.6 %copy-start = (bf16[4,1,80,2,1536]{4,3,2,1,0:T(2,128)(2,1)S(1)}, bf16[4,1,80,2,1536]{4,3,2,1,0:T(2,128)(2,1)}, u32[]{:S(2)}) copy-start(bf16[4,1,80,2,1536]{4,3,2,1,0:T(2,128)(2,1)} %param.26) | copy-start | bytes 5898244
  0.6 5.4 %copy-start.18 = (f32[128,256]{1,0:T(8,128)S(1)}, f32[128,256]{1,0:T(8,128)}, u32[]{:S(2)}) copy-start(f32[128,256]{1,0:T(8,128)} %param.31) | copy-start | bytes 393220
  0.7 5.4 %copy-start.19 = (s32[128]{0:T(128)S(1)}, s32[128]{0:T(128)}, u32[]{:S(2)}) copy-start(s32[128]{0:T(128)} %param.32) | copy-start | bytes 1540
  0.9 5.3 %copy-start.1 = (bf16[128,40,256]{2,1,0:T(8,128)(2,1)S(1)}, bf16[128,40,256]{2,1,0:T(8,128)(2,1)}, u32[]{:S(2)}) copy-start(bf16[128,40,256]{2,1,0:T(8,128)(2,1)} %param.30) | copy-start | bytes 7864324
  2.2 4.7 %copy-start.20 = (s32[128]{0:T(128)S(1)}, s32[128]{0:T(128)}, u32[]{:S(2)}) copy-start(s32[128]{0:T(128)} %param.33) | copy-start | bytes 1540
  2.2 4.7 %copy-start.21 = (f32[8]{0:T(128)S(1)}, f32[8]{0:T(128)}, u32[]{:S(2)}) copy-start(f32[8]{0:T(128)} %param.34) | copy-start | bytes 100
  2.9 4.4 %collective-permute-start.48 = (f32[16,80]{1,0:T(8,128)S(1)}, f32[16,80]{1,0:T(8,128)S(1)}, u32[]{:S(2)}, u32[]{:S(2)}) collective-permute-start(f32[16,80]{1,0:T(8,128)S(1)} %broadcast_select_fusion), channel_id=1, source_target_pairs={{0,1},{1,0},{2,3},{3,2},{4,5},{5,4},{6,7},{7,6},{8,9},{9,8},{10,11... | collective-permute-start | bytes 15368 | tf_op jit(solution)/shard_map/ppermute | solution.py:19
  5.5 14.5 %collective-permute-start.54 = (bf16[16,40,256]{2,1,0:T(8,128)(2,1)S(1)}, bf16[16,40,256]{2,1,0:T(8,128)(2,1)S(1)}, u32[]{:S(2)}, u32[]{:S(2)}) collective-permute-start(bf16[16,40,256]{2,1,0:T(8,128)(2,1)S(1)} %slice.422), channel_id=1, source_target_pairs={{0,1},{1,0},{2,3},{3,2},{4,5},{5,4},{6,7},{7,6},{8,9},{9,8},{10,11... | collective-permute-start | bytes 983048 | tf_op jit(solution)/shard_map/ppermute | solution.py:101
  7.6 2.0 %collective-permute-start.49 = (f32[24,80]{1,0:T(8,128)S(1)}, f32[24,80]{1,0:T(8,128)S(1)}, u32[]{:S(2)}, u32[]{:S(2)}) collective-permute-start(f32[24,80]{1,0:T(8,128)S(1)} %select_maximum_fusion), channel_id=1, source_target_pairs={{0,2},{2,0},{4,6},{6,4},{8,10},{10,8},{12,14},{14,12},{16,18},{18,... | collective-permute-start | bytes 23048 | tf_op jit(solution)/shard_map/ppermute | solution.py:19
  7.6 3.9 %collective-permute-start.50 = (f32[24,80]{1,0:T(8,128)S(1)}, f32[24,80]{1,0:T(8,128)S(1)}, u32[]{:S(2)}, u32[]{:S(2)}) collective-permute-start(f32[24,80]{1,0:T(8,128)S(1)} %select_maximum_fusion), channel_id=1, source_target_pairs={{0,4},{2,6},{4,0},{6,2},{8,12},{10,14},{12,8},{14,10},{16,20},{18,... | collective-permute-start | bytes 23048 | tf_op jit(solution)/shard_map/ppermute | solution.py:19
  8.2 3.3 %collective-permute-start.51 = (f32[24,80]{1,0:T(8,128)S(1)}, f32[24,80]{1,0:T(8,128)S(1)}, u32[]{:S(2)}, u32[]{:S(2)}) collective-permute-start(f32[24,80]{1,0:T(8,128)S(1)} %select_maximum_fusion), channel_id=1, source_target_pairs={{0,6},{2,4},{4,2},{6,0},{8,14},{10,12},{12,10},{14,8},{16,22},{18,... | collective-permute-start | bytes 23048 | tf_op jit(solution)/shard_map/ppermute | solution.py:19
  11.5 3.8 %collective-permute-start.52 = (f32[24,80]{1,0:T(8,128)S(1)}, f32[24,80]{1,0:T(8,128)S(1)}, u32[]{:S(2)}, u32[]{:S(2)}) collective-permute-start(f32[24,80]{1,0:T(8,128)S(1)} %add_add_fusion), channel_id=1, source_target_pairs={{0,8},{2,10},{4,12},{6,14},{8,0},{10,2},{12,4},{14,6},{16,24},{18,... | collective-permute-start | bytes 23048 | tf_op jit(solution)/shard_map/ppermute | solution.py:19
  15.3 4.6 %collective-permute-start.53 = (f32[24,80]{1,0:T(8,128)S(1)}, f32[24,80]{1,0:T(8,128)S(1)}, u32[]{:S(2)}, u32[]{:S(2)}) collective-permute-start(f32[24,80]{1,0:T(8,128)S(1)} %add.304), channel_id=1, source_target_pairs={{0,16},{2,18},{4,20},{6,22},{8,24},{10,26},{12,28},{14,30},{16,0},... | collective-permute-start | bytes 23048 | tf_op jit(solution)/shard_map/ppermute | solution.py:19
  20.1 7.3 %collective-permute-start.21 = (bf16[28,8,256]{2,1,0:T(8,128)(2,1)S(1)}, bf16[28,8,256]{2,1,0:T(8,128)(2,1)S(1)}, u32[]{:S(2)}, u32[]{:S(2)}) collective-permute-start(bf16[28,8,256]{2,1,0:T(8,128)(2,1)S(1)} %fusion.95), channel_id=1, source_target_pairs={{0,1},{1,0},{2,3},{3,2},{4,5},{5,4},{6,7},{7,6},{8,9},{9,8},{10,11... | collective-permute-start | bytes 344072 | tf_op jit(solution)/shard_map/cond/branch_8_fun/ppermute | solution.py:185
  21.9 5.7 %collective-permute-start.22 = (bf16[28,8,256]{2,1,0:T(8,128)(2,1)S(1)}, bf16[28,8,256]{2,1,0:T(8,128)(2,1)S(1)}, u32[]{:S(2)}, u32[]{:S(2)}) collective-permute-start(bf16[28,8,256]{2,1,0:T(8,128)(2,1)S(1)} %fusion.96), channel_id=1, source_target_pairs={{0,1},{1,0},{2,3},{3,2},{4,5},{5,4},{6,7},{7,6},{8,9},{9,8},{10,11... | collective-permute-start | bytes 344072 | tf_op jit(solution)/shard_map/cond/branch_8_fun/ppermute | solution.py:185
  22.6 4.2 %collective-permute-start.23 = (f32[8,8]{1,0:T(8,128)S(1)}, f32[8,8]{1,0:T(8,128)S(1)}, u32[]{:S(2)}, u32[]{:S(2)}) collective-permute-start(f32[8,8]{1,0:T(8,128)S(1)} %fusion.257), channel_id=1, source_target_pairs={{0,1},{1,0},{2,3},{3,2},{4,5},{5,4},{6,7},{7,6},{8,9},{9,8},{10,11... | collective-permute-start | bytes 776 | tf_op jit(solution)/shard_map/cond/branch_8_fun/ppermute | solution.py:177
  27.6 1.0 %copy-start.9 = (f32[128,8,256]{2,1,0:T(8,128)}, f32[128,8,256]{2,1,0:T(8,128)S(1)}, u32[]{:S(2)}) copy-start(f32[128,8,256]{2,1,0:T(8,128)S(1)} %fusion.100) | copy-start | bytes 3145732 | tf_op jit(solution)/shard_map/cond
